TPU v7x, 256 devices: a whole 4x4x8 slice. The times are simulated.
256 devices in a mesh: col: 64 (over z, x, core), row: 4 (over y).
Axes of the slice: x: 4, y: 4, z: 8, core: 2. Of those that a mesh axis runs over, the one named last changes fastest.
Arguments:
- slab: float32 [1024, 262144], P('row', 'col'), may hold values from -6 to 6
- omega: float32 [262144, 256], P('col'), may hold values from -0.01171875 to 0.01171875
- y_prev: float32 [65536, 256], P(('row', 'col')), may hold values from -0.6 to 0.6
- w_prev: float32 [512, 262144], P('row', 'col'), may hold values from -6 to 6
- prev_bucket: int32 [65536], P(('row', 'col')), may hold values from 0 to 511
- prev_sign: int32 [65536], P(('row', 'col')), may hold values from 0 to 1
- slab_bucket: int32 [1024], P('row'), may hold values from 0 to 511
- slab_sign: int32 [1024], P('row'), may hold values from 0 to 1
Outputs:
- q_prev: float32 [65536, 256], P(('row', 'col'))
- q_slab: float32 [1024, 256], P(('row', 'col'))
- x_core: float32 [256, 262144], P('row', 'col')
All inputs are finite; a program needn't handle non-finite values.
Results may differ from a plain program's by a relative error of at most 0.00016.
Values sent between devices are 32-bit elements; how exact they have to be, the bound alone decides.
A program may use at most 64 MiB of HBM per device.

v0:
```python
import jax
import jax.numpy as jnp
from jax import lax
from jax.experimental import pallas as pl
from jax.experimental.pallas import tpu as pltpu
from jax.sharding import Mesh
from jax.sharding import PartitionSpec as P

L = 512
COL = ("col_0", "col_1", "col_2")
ROW_COL = ("row", "col_0", "col_1", "col_2")


highest = lax.Precision.HIGHEST


def in_blocks(x, dim, size):
    before, after = (x.shape[:dim], x.shape[dim + 1 :])
    return jnp.moveaxis(x.reshape(*before, size, -1, *after), dim, 0)


def sum_at_owner(x, axis, dim):
    size = lax.axis_size(axis)
    blocks = lax.all_to_all(in_blocks(x, dim, size), axis, 0, 0, tiled=True)
    return jnp.sum(blocks, axis=0)


def sum_in_two_steps(x, axes, dim):
    far, near = axes
    blocks = in_blocks(x, dim, lax.axis_size(far))
    nearer = sum_at_owner(blocks, near, dim + 1)
    arrived = lax.all_to_all(nearer, far, split_axis=0, concat_axis=0, tiled=True)
    return arrived.sum(axis=0)


def filled_up(lines, size):
    spare = -lines.shape[0] % size
    if not spare:
        return lines
    return jnp.concatenate([lines, jnp.zeros((spare, *lines.shape[1:]), lines.dtype)])


def from_everyone(x, axis):
    copies = jnp.broadcast_to(x, (lax.axis_size(axis), *x.shape))
    return lax.all_to_all(copies, axis, split_axis=0, concat_axis=0, tiled=True)


def in_order(blocks, dim):
    shape = list(blocks.shape[1:])
    shape[dim] *= blocks.shape[0]
    return jnp.moveaxis(blocks, 0, dim).reshape(shape)


def gathered_by_axis(x, axes, dim):
    far, near = axes
    blocks = from_everyone(from_everyone(x, far), near)
    return in_order(blocks.swapaxes(0, 1).reshape(-1, *x.shape), dim)


def sum_by_parts(x, axes):
    lines = x.reshape(-1, x.shape[-1])
    own = sum_in_two_steps(
        filled_up(lines, lax.axis_size(axes[0]) * lax.axis_size(axes[1])), axes, 0
    )
    whole = gathered_by_axis(own, axes, 0)
    return whole[: len(lines)].reshape(x.shape)


def matmul(left, right):
    return jnp.dot(left, right, precision=highest, preferred_element_type=jnp.float32)


def signed_table(bucket, sign, height):
    levels = lax.broadcasted_iota(jnp.int32, (height, bucket.shape[0]), 0)
    signs = (2 * sign - 1).astype(jnp.float32)
    return jnp.where(levels == bucket[None, :], signs[None, :], 0.0)


K = 256
BLK = 16
SUP = 64


def mm(a, b, dims=((1,), (0,))):
    return lax.dot_general(a, b, (dims, ((), ())), precision=highest, preferred_element_type=jnp.float32)


def eliminate(panel, k):
    off = k * BLK
    tile = off // 128 * 128
    cols = []
    for j in range(BLK):
        c = off + j
        cols.append([jnp.broadcast_to(panel[h * 8 : h * 8 + 8, c : c + 1], (8, 128)) for h in (0, 1)])
    lane = lax.broadcasted_iota(jnp.int32, (8, K), 1)
    row = lax.broadcasted_iota(jnp.int32, (8, K), 0)
    row1 = lax.broadcasted_iota(jnp.int32, (8, 128), 0)
    inside = (lane >= off) & (lane < off + BLK)
    top = jnp.where(inside, (lane == row + off).astype(jnp.float32), panel[:8])
    bot = jnp.where(inside, (lane == row + off + 8).astype(jnp.float32), panel[8:])
    lane1 = lax.broadcasted_iota(jnp.int32, (8, 128), 1) + tile
    corner = [jnp.zeros((8, 128), jnp.float32), jnp.zeros((8, 128), jnp.float32)]
    scales = []
    for j in range(BLK):
        h, r = divmod(j, 8)
        mine = cols[j]
        pivot = jnp.broadcast_to(mine[h][r : r + 1], (8, 128))
        rs = lax.rsqrt(pivot)
        inv = rs * rs
        scales.append(rs)
        low = mine[1] * inv
        high = None
        if h == 0:
            high = mine[0] * inv
        for m in range(j + 1, BLK):
            hm, rm = divmod(m, 8)
            u = jnp.broadcast_to(mine[hm][rm : rm + 1], (8, 128))
            cols[m][1] = cols[m][1] - low * u
            if hm == 0:
                cols[m][0] = cols[m][0] - high * u
        if h == 0:
            p = jnp.broadcast_to(top[r : r + 1], (8, K))
            hm_ = jnp.where(row1 > r, high, 0.0)
            top = top - jnp.concatenate([hm_, hm_], axis=1) * p
            bot = bot - jnp.concatenate([low, low], axis=1) * p
        else:
            p = jnp.broadcast_to(bot[r : r + 1], (8, K))
            lm_ = jnp.where(row1 > r, low, 0.0)
            bot = bot - jnp.concatenate([lm_, lm_], axis=1) * p
    st = jnp.zeros((8, 128), jnp.float32)
    sb = jnp.zeros((8, 128), jnp.float32)
    for j in range(8):
        st = jnp.where(row1 == j, scales[j], st)
        sb = jnp.where(row1 == j, scales[j + 8], sb)
    top = top * jnp.concatenate([st, st], axis=1)
    bot = bot * jnp.concatenate([sb, sb], axis=1)
    for j in range(BLK):
        for h in (0, 1):
            keep = (lane1 == off + j) & (row1 + 8 * h >= j)
            corner[h] = jnp.where(keep, cols[j][h] * scales[j], corner[h])
    return jnp.concatenate([top, bot], axis=0), jnp.concatenate(corner, axis=0)


def factor_step(w, u, k):
    off = k * BLK
    rows = slice(off, off + BLK)
    panel, corner = eliminate(w[rows, :], k)
    tile = off // 128 * 128
    w[rows, :] = panel
    lane = lax.broadcasted_iota(jnp.int32, (BLK, K), 1)
    upper = jnp.where(lane >= off + BLK, panel, 0.0)
    u[rows, :] = upper
    sup_end = (off // SUP + 1) * SUP
    if off + BLK < sup_end:
        turned = panel[:, tile : tile + 128].T
        left = turned[off + BLK - tile : sup_end - tile]
        rest = slice(off + BLK, sup_end)
        lane2 = lax.broadcasted_iota(jnp.int32, (sup_end - off - BLK, K), 1)
        old = jnp.where((lane2 >= off) & (lane2 < off + BLK), 0.0, w[rest, :])
        w[rest, :] = old - mm(left, panel)
    elif sup_end < K:
        start = sup_end - SUP
        block = w[start:sup_end, :]
        t0 = sup_end // 128 * 128
        turned = block[:, t0:].T
        left = turned[sup_end - t0 :]
        rest = slice(sup_end, K)
        lane2 = lax.broadcasted_iota(jnp.int32, (K - sup_end, K), 1)
        old = jnp.where((lane2 >= start) & (lane2 < sup_end), 0.0, w[rest, :])
        lane3 = lax.broadcasted_iota(jnp.int32, (SUP, K), 1)
        row3 = lax.broadcasted_iota(jnp.int32, (SUP, K), 0) + start
        block = jnp.where((lane3 < sup_end) & (lane3 > row3), 0.0, block)
        w[rest, :] = old - mm(left, block)
    return corner


def factor_both(wg, ws, ug, us):
    for k in range(K // BLK):
        cg = factor_step(wg, ug, k)
        factor_step(ws, us, k)
        off = k * BLK
        tile = off // 128 * 128
        rows = slice(off, off + BLK)
        turned = cg.T[off - tile : off - tile + BLK]
        ug[rows, off:off + BLK] = turned


def factors_kernel(gram, sketch, xg, mapping, u, xs, us):
    xg[...] = gram[...]
    xs[...] = mm(sketch[...], sketch[...], ((0,), (0,)))
    factor_both(xg, xs, u, us)
    row = lax.broadcasted_iota(jnp.int32, (K, K), 0)
    lane = lax.broadcasted_iota(jnp.int32, (K, K), 1)
    xg[...] = jnp.where(lane <= row, xg[...], 0.0)
    inner = jnp.where(lane <= row, xs[...], 0.0)
    core = mm(mm(u[...], inner, ((1,), (1,))), inner)
    mapping[...] = mm(core, sketch[...], ((1,), (1,)))


def factors(gram, sketch):
    vmem = pl.BlockSpec(memory_space=pltpu.VMEM)
    return pl.pallas_call(
        factors_kernel,
        out_shape=(
            jax.ShapeDtypeStruct((K, K), jnp.float32),
            jax.ShapeDtypeStruct((K, L), jnp.float32),
        ),
        in_specs=[vmem] * 2,
        out_specs=[vmem] * 2,
        scratch_shapes=[pltpu.VMEM((K, K), jnp.float32)] * 3,
        cost_estimate=pl.CostEstimate(flops=12_000_000_000, bytes_accessed=2_000_000, transcendentals=0),
        name="factors",
    )(gram, sketch)


def on_device(slab, omega, y_prev, w_prev, prev_bucket, prev_sign, slab_bucket, slab_sign):
    col_count = lax.axis_size(COL)
    col_place = lax.axis_index(COL)
    row_place = lax.axis_index("row")
    share = slab.shape[0] // col_count
    y_new = sum_in_two_steps(matmul(slab, omega), (("col_0", "col_1"), "col_2"), 0)
    leaf = jnp.concatenate([y_prev, y_new], axis=0)
    own_bucket = jnp.concatenate(
        [prev_bucket, lax.dynamic_slice_in_dim(slab_bucket, col_place * share, share, 0)]
    )
    own_sign = jnp.concatenate(
        [prev_sign, lax.dynamic_slice_in_dim(slab_sign, col_place * share, share, 0)]
    )
    local_table = signed_table(own_bucket, own_sign, L)
    both = jnp.concatenate([matmul(local_table, leaf), matmul(leaf.T, leaf)], axis=0)
    both = sum_by_parts(both, (("col_0", "col_1"), ("col_2", "row")))
    inverse, mapping = factors(both[L:], both[:L])
    q_leaf = matmul(leaf, inverse.T)
    lshare = w_prev.shape[0]
    own_cols = lax.dynamic_slice_in_dim(mapping, row_place * lshare, lshare, 1)
    slab_table = signed_table(slab_bucket, slab_sign, L)
    combined = matmul(mapping, slab_table)
    first = matmul(combined, slab)
    x_core = sum_at_owner(first + matmul(own_cols, w_prev), "row", 0)
    return (q_leaf[: y_prev.shape[0]], q_leaf[y_prev.shape[0] :], x_core)


def solution(mesh):
    finer = Mesh(
        mesh.devices.reshape(8, 4, 2, mesh.shape["row"]), ("col_0", "col_1", "col_2", "row")
    )
    return jax.shard_map(
        on_device,
        mesh=finer,
        in_specs=(
            P("row", COL),
            P(COL, None),
            P(ROW_COL, None),
            P("row", COL),
            P(ROW_COL),
            P(ROW_COL),
            P("row"),
            P("row"),
        ),
        out_specs=(P(ROW_COL, None), P(ROW_COL, None), P("row", COL)),
        check_vma=False,
    )
```

profile of v0, /device:TPU:1, one launch (start us, length us, event | category | flops | bytes accessed | tf_op | source)
XLA Modules:
  0.0 194.5 jit_solution(10116415132343724412)
XLA Ops:
  0.6 0.0 copy-start
  0.6 0.0 copy-start.4
  0.7 0.0 copy-start.7
  0.7 0.0 copy-start.6
  0.7 0.0 copy-start.5
  0.7 0.0 copy-start.2
  0.7 7.2 %fusion.21 = f32[256,256]{1,0:T(8,128)S(1)} fusion(f32[256,4096]{1,0:T(8,128)} %param.8, f32[4096,256]{1,0:T(8,128)} %param.9), kind=kOutput, calls=%fused_computation.30 | convolution fusion | flops 3221225472 | bytes 8650752 | tf_op jit(solution)/shard_map/dot_general | solution.py:70
  7.9 0.1 reshape_reshape.9
  8.0 6.8 %all_to_all.35 = f32[2,32,4,256]{3,2,1,0:T(4,128)S(1)} all-to-all(f32[2,32,4,256]{3,2,1,0:T(4,128)S(1)} %bitcast.16), channel_id=1, replica_groups=mesh['col_0'=8,'col_1'=4,'col_2'=2,'row'=4] {'col_2'}, dimensions={0} | all-to-all | bytes 524288 | tf_op jit(solution)/shard_map/all_to_all | solution.py:24
  14.8 0.7 reduce_sum.45
  15.5 9.3 %all-to-all-start.1 = ((f32[32,4,256]{2,1,0:T(4,128)}), f32[32,4,256]{2,1,0:T(4,128)S(1)}, u32[]{:S(2)}, u32[]{:S(2)}) async-start(f32[32,4,256]{2,1,0:T(4,128)} %reduce_sum.45), calls=%async_computation.1 | async-start | bytes 262144 | tf_op jit(solution)/shard_map/all_to_all | solution.py:32
  24.9 0.0 copy-done.4
  24.9 0.1 dynamic_slice.9
  25.0 0.0 copy-done.7
  25.0 0.1 dynamic_slice.10
  25.0 0.0 copy-done.6
  25.0 0.0 copy-done.5
  25.0 9.2 %all-to-all-done.1 = f32[32,4,256]{2,1,0:T(4,128)S(1)} async-done(((f32[32,4,256]{2,1,0:T(4,128)}), f32[32,4,256]{2,1,0:T(4,128)S(1)}, u32[]{:S(2)}, u32[]{:S(2)}) %all-to-all-start.1) | async-done | bytes 131104 | tf_op jit(solution)/shard_map/all_to_all | solution.py:32
  34.3 0.0 copy-done.2
  34.3 0.8 fusion.11
  35.1 1.0 fusion
  36.1 0.9 pad_maximum_fusion
  37.0 1.5 reshape_reshape.10
  38.5 0.5 copy.30
  39.0 18.5 %all_to_all.36 = f32[8,32,3,256]{3,1,2,0:T(8,128)S(1)} all-to-all(f32[8,32,3,256]{3,1,2,0:T(8,128)S(1)} %copy.30), channel_id=1, replica_groups=mesh['col_0'=8,'col_1'=4,'col_2'=2,'row'=4] {'col_2','row'}, dimensions={0} | all-to-all | bytes 1572864 | tf_op jit(solution)/shard_map/all_to_all | solution.py:24
  57.5 0.1 reduce_sum.47
  57.5 0.1 copy.31
  57.6 12.4 %all_to_all.37 = f32[32,3,256]{2,1,0:T(4,128)S(1)} all-to-all(f32[32,3,256]{2,1,0:T(4,128)S(1)} %copy.31), channel_id=1, replica_groups=mesh['col_0'=8,'col_1'=4,'col_2'=2,'row'=4] {'col_0','col_1'}, dimensions={0} | all-to-all | bytes 196608 | tf_op jit(solution)/shard_map/all_to_all | solution.py:32
  70.0 13.1 %all_to_all.38 = f32[32,3,256]{2,1,0:T(4,128)S(1)} all-to-all(f32[32,3,256]{2,1,0:T(4,128)S(1)} %broadcast_in_dim.36), channel_id=1, replica_groups=mesh['col_0'=8,'col_1'=4,'col_2'=2,'row'=4] {'col_0','col_1'}, dimensions={0} | all-to-all | bytes 196608 | tf_op jit(solution)/shard_map/all_to_all | solution.py:45
  83.1 1.0 broadcast_in_dim.37
  84.1 6.3 %all-to-all-start.5 = ((f32[8,32,3,256]{3,1,2,0:T(8,128)}), f32[8,32,3,256]{3,1,2,0:T(8,128)S(1)}, u32[]{:S(2)}, u32[]{:S(2)}) async-start(f32[8,32,3,256]{3,1,2,0:T(8,128)} %broadcast_in_dim.37), calls=%async_computation.5 | async-start | bytes 1572864 | tf_op jit(solution)/shard_map/all_to_all | solution.py:45
  90.4 12.2 %all-to-all-done.5 = f32[8,32,3,256]{3,1,2,0:T(8,128)S(1)} async-done(((f32[8,32,3,256]{3,1,2,0:T(8,128)}), f32[8,32,3,256]{3,1,2,0:T(8,128)S(1)}, u32[]{:S(2)}, u32[]{:S(2)}) %all-to-all-start.5) | async-done | bytes 786464 | tf_op jit(solution)/shard_map/all_to_all | solution.py:45
  102.6 0.9 copy-done.1
  103.4 1.7 copy.33
  105.1 1.3 reshape_reshape.11
  106.4 1.7 slice.16.gram
  108.1 1.9 slice.17.sketch
  109.9 14.2 %factors.1 = (f32[256,256]{1,0:T(8,128)}, f32[256,512]{1,0:T(8,128)}) custom-call(f32[256,256]{1,0:T(8,128)} %slice.16.gram, f32[512,256]{1,0:T(8,128)} %slice.17.sketch), custom_call_target="tpu_custom_call" | custom-call | flops 12000000000 | bytes 2000000 | tf_op jit(solution)/shard_map/factors/pallas_call | solution.py:202
  124.1 1.7 fusion.2
  125.8 5.7 %fusion.22 = f32[256,4096]{1,0:T(8,128)S(1)} fusion(f32[256,256]{1,0:T(8,128)S(1)} %fusion.2, f32[256,4096]{1,0:T(8,128)} %param.8), kind=kOutput, calls=%fused_computation.31 | convolution fusion | flops 3221225472 | bytes 8650752 | tf_op jit(solution)/shard_map/dot_general | solution.py:70
  131.4 0.0 copy-done
  131.4 6.0 %convolution_add_fusion = f32[256,4096]{1,0:T(8,128)} fusion(f32[256,4096]{1,0:T(8,128)S(1)} %fusion.22, f32[128,4096]{1,0:T(8,128)S(1)} %copy-done, f32[256,512]{1,0:T(8,128)} %get-tuple-element.6, s32[]{:T(128)S(6)} %select_n.18), kind=kOutput, calls=%fused_computation | convolution fusion | flops 1611661312 | bytes 10616836 | tf_op jit(solution)/shard_map/dot_general | solution.py:70
  137.4 5.0 %all-to-all-start.6 = ((f32[4,64,4096]{2,1,0:T(8,128)}), f32[4,64,4096]{2,1,0:T(8,128)}, u32[]{:S(2)}, u32[]{:S(2)}) async-start(f32[4,64,4096]{2,1,0:T(8,128)} %bitcast.13), calls=%async_computation.6 | async-start | bytes 8388608 | tf_op jit(solution)/shard_map/all_to_all | solution.py:24
  142.4 0.4 fusion.10
  142.8 0.6 slice.19
  143.4 0.7 slice.18
  144.1 46.9 %all-to-all-done.6 = f32[4,64,4096]{2,1,0:T(8,128)} async-done(((f32[4,64,4096]{2,1,0:T(8,128)}), f32[4,64,4096]{2,1,0:T(8,128)}, u32[]{:S(2)}, u32[]{:S(2)}) %all-to-all-start.6) | async-done | bytes 4194336 | tf_op jit(solution)/shard_map/all_to_all | solution.py:24
  191.0 3.5 %reduce_sum.49 = f32[64,4096]{1,0:T(8,128)} reduce(f32[4,64,4096]{2,1,0:T(8,128)} %all-to-all-done.6, f32[]{:T(128)} %constant.14.clone.1), dimensions={0}, to_apply=%region_4.5 | reduce | flops 786432 | bytes 5242884 | tf_op jit(solution)/shard_map/reduce_sum | solution.py:25
  (10 shorter events, 0.2 us)
Async XLA Ops:
  0.6 130.8 %copy-start = (f32[128,4096]{1,0:T(8,128)S(1)}, f32[128,4096]{1,0:T(8,128)}, u32[]{:S(2)}) copy-start(f32[128,4096]{1,0:T(8,128)} %param.11) | copy-start | bytes 6291460
  0.6 24.2 %copy-start.4 = (s32[256]{0:T(256)S(1)}, s32[256]{0:T(256)}, u32[]{:S(2)}) copy-start(s32[256]{0:T(256)} %param.14) | copy-start | bytes 3076
  0.7 24.3 %copy-start.7 = (s32[256]{0:T(256)S(1)}, s32[256]{0:T(256)}, u32[]{:S(2)}) copy-start(s32[256]{0:T(256)} %param.15) | copy-start | bytes 3076
  0.7 24.4 %copy-start.6 = (s32[256]{0:T(256)S(1)}, s32[256]{0:T(256)}, u32[]{:S(2)}) copy-start(s32[256]{0:T(256)} %param.13) | copy-start | bytes 3076
  0.7 24.4 %copy-start.5 = (s32[256]{0:T(256)S(1)}, s32[256]{0:T(256)}, u32[]{:S(2)}) copy-start(s32[256]{0:T(256)} %param.12) | copy-start | bytes 3076
  0.7 33.6 %copy-start.2 = (f32[256,256]{1,0:T(8,128)S(1)}, f32[256,256]{1,0:T(8,128)}, u32[]{:S(2)}) copy-start(f32[256,256]{1,0:T(8,128)} %param.10) | copy-start | bytes 786436
  15.5 18.7 %all-to-all-start.1 = ((f32[32,4,256]{2,1,0:T(4,128)}), f32[32,4,256]{2,1,0:T(4,128)S(1)}, u32[]{:S(2)}, u32[]{:S(2)}) async-start(f32[32,4,256]{2,1,0:T(4,128)} %reduce_sum.45), calls=%async_computation.1 | async-start | bytes 262144 | tf_op jit(solution)/shard_map/all_to_all | solution.py:32
  84.1 18.5 %all-to-all-start.5 = ((f32[8,32,3,256]{3,1,2,0:T(8,128)}), f32[8,32,3,256]{3,1,2,0:T(8,128)S(1)}, u32[]{:S(2)}, u32[]{:S(2)}) async-start(f32[8,32,3,256]{3,1,2,0:T(8,128)} %broadcast_in_dim.37), calls=%async_computation.5 | async-start | bytes 1572864 | tf_op jit(solution)/shard_map/all_to_all | solution.py:45
  102.6 0.9 copy-start.1
  137.4 5.0 %copy-start.3 = (f32[256,256]{1,0:T(8,128)S(1)}, f32[256,256]{1,0:T(8,128)}, u32[]{:S(2)}) copy-start(f32[256,256]{1,0:T(8,128)} %get-tuple-element.5) | copy-start | bytes 786436
  137.4 53.6 %all-to-all-start.6 = ((f32[4,64,4096]{2,1,0:T(8,128)}), f32[4,64,4096]{2,1,0:T(8,128)}, u32[]{:S(2)}, u32[]{:S(2)}) async-start(f32[4,64,4096]{2,1,0:T(8,128)} %bitcast.13), calls=%async_computation.6 | async-start | bytes 8388608 | tf_op jit(solution)/shard_map/all_to_all | solution.py:24
where the time goes:
time: 195 us
  waiting for transfers between devices  68.2 us (35%)
  blocking collectives  50.7 us (26%)
  matrix products  22.7 us (12%)
  starting transfers between devices  20.6 us (11%)
  Pallas kernels  14.2 us (7%)
  local copies, waits for them, and re-layouts  11.9 us (6%)
  other arithmetic  5.31 us (3%)
    all_to_all x1, waiting for transfers between devices, sum_at_owner(): blocks = lax.all_to_all(in_blocks(x, dim, size), axis, 0, 0, tiled=True)  46.9 us
    all_to_all x2, blocking collectives, sum_at_owner(): blocks = lax.all_to_all(in_blocks(x, dim, size), axis, 0, 0, tiled=True)  25.3 us
    dot_general x7, matrix products, matmul(): jnp.dot(left, right, precision=highest, preferred_element_type=jnp.float32)  22.7 us
    pallas_call x1, Pallas kernels, factors(): pl.pallas_call(factors_kernel, out_shape=(jax.ShapeDtypeStruct((K, K), jn...  14.2 us
    all_to_all x1, blocking collectives, from_everyone(): return lax.all_to_all(copies, axis, split_axis=0, concat_axis=0, tiled=True)  13.1 us
    all_to_all x1, blocking collectives, sum_in_two_steps(): lax.all_to_all(nearer, far, split_axis=0, concat_axis=0, tiled=True)  12.4 us
    all_to_all x1, waiting for transfers between devices, from_everyone(): return lax.all_to_all(copies, axis, split_axis=0, concat_axis=0, tiled=True)  12.2 us
    all_to_all x1, starting transfers between devices, sum_in_two_steps(): lax.all_to_all(nearer, far, split_axis=0, concat_axis=0, tiled=True)  9.33 us
  transfers between devices with their start and end apart: 3, of which 3 were waited for; matrix products, arithmetic and copies ran while one was open for 1% of the time, Pallas kernels for 0%

commit v1 on v0

v1 whole, which is shorter than its diff:
```python
import functools

import jax
import jax.numpy as jnp
from jax import lax
from jax.experimental import pallas as pl
from jax.experimental.pallas import tpu as pltpu
from jax.sharding import Mesh
from jax.sharding import PartitionSpec as P

L = 512
COL = ("z", "x", "core")
ROW_COL = ("y", "z", "x", "core")
MESH = pl.DeviceIdType.MESH
highest = lax.Precision.HIGHEST
K = 256
BLK = 16
SUP = 64


def mm(a, b, dims=((1,), (0,))):
    return lax.dot_general(a, b, (dims, ((), ())), precision=highest, preferred_element_type=jnp.float32)


def eliminate(panel, k):
    off = k * BLK
    tile = off // 128 * 128
    cols = []
    for j in range(BLK):
        c = off + j
        cols.append([jnp.broadcast_to(panel[h * 8 : h * 8 + 8, c : c + 1], (8, 128)) for h in (0, 1)])
    lane = lax.broadcasted_iota(jnp.int32, (8, K), 1)
    row = lax.broadcasted_iota(jnp.int32, (8, K), 0)
    row1 = lax.broadcasted_iota(jnp.int32, (8, 128), 0)
    inside = (lane >= off) & (lane < off + BLK)
    top = jnp.where(inside, (lane == row + off).astype(jnp.float32), panel[:8])
    bot = jnp.where(inside, (lane == row + off + 8).astype(jnp.float32), panel[8:])
    lane1 = lax.broadcasted_iota(jnp.int32, (8, 128), 1) + tile
    corner = [jnp.zeros((8, 128), jnp.float32), jnp.zeros((8, 128), jnp.float32)]
    scales = []
    for j in range(BLK):
        h, r = divmod(j, 8)
        mine = cols[j]
        pivot = jnp.broadcast_to(mine[h][r : r + 1], (8, 128))
        rs = lax.rsqrt(pivot)
        inv = rs * rs
        scales.append(rs)
        low = mine[1] * inv
        high = None
        if h == 0:
            high = mine[0] * inv
        for m in range(j + 1, BLK):
            hm, rm = divmod(m, 8)
            u = jnp.broadcast_to(mine[hm][rm : rm + 1], (8, 128))
            cols[m][1] = cols[m][1] - low * u
            if hm == 0:
                cols[m][0] = cols[m][0] - high * u
        if h == 0:
            p = jnp.broadcast_to(top[r : r + 1], (8, K))
            hm_ = jnp.where(row1 > r, high, 0.0)
            top = top - jnp.concatenate([hm_, hm_], axis=1) * p
            bot = bot - jnp.concatenate([low, low], axis=1) * p
        else:
            p = jnp.broadcast_to(bot[r : r + 1], (8, K))
            lm_ = jnp.where(row1 > r, low, 0.0)
            bot = bot - jnp.concatenate([lm_, lm_], axis=1) * p
    st = jnp.zeros((8, 128), jnp.float32)
    sb = jnp.zeros((8, 128), jnp.float32)
    for j in range(8):
        st = jnp.where(row1 == j, scales[j], st)
        sb = jnp.where(row1 == j, scales[j + 8], sb)
    top = top * jnp.concatenate([st, st], axis=1)
    bot = bot * jnp.concatenate([sb, sb], axis=1)
    for j in range(BLK):
        for h in (0, 1):
            keep = (lane1 == off + j) & (row1 + 8 * h >= j)
            corner[h] = jnp.where(keep, cols[j][h] * scales[j], corner[h])
    return jnp.concatenate([top, bot], axis=0), jnp.concatenate(corner, axis=0)


def factor_step(w, u, k):
    off = k * BLK
    rows = slice(off, off + BLK)
    panel, corner = eliminate(w[rows, :], k)
    tile = off // 128 * 128
    w[rows, :] = panel
    lane = lax.broadcasted_iota(jnp.int32, (BLK, K), 1)
    upper = jnp.where(lane >= off + BLK, panel, 0.0)
    u[rows, :] = upper
    sup_end = (off // SUP + 1) * SUP
    if off + BLK < sup_end:
        turned = panel[:, tile : tile + 128].T
        left = turned[off + BLK - tile : sup_end - tile]
        rest = slice(off + BLK, sup_end)
        lane2 = lax.broadcasted_iota(jnp.int32, (sup_end - off - BLK, K), 1)
        old = jnp.where((lane2 >= off) & (lane2 < off + BLK), 0.0, w[rest, :])
        w[rest, :] = old - mm(left, panel)
    elif sup_end < K:
        start = sup_end - SUP
        block = w[start:sup_end, :]
        t0 = sup_end // 128 * 128
        turned = block[:, t0:].T
        left = turned[sup_end - t0 :]
        rest = slice(sup_end, K)
        lane2 = lax.broadcasted_iota(jnp.int32, (K - sup_end, K), 1)
        old = jnp.where((lane2 >= start) & (lane2 < sup_end), 0.0, w[rest, :])
        lane3 = lax.broadcasted_iota(jnp.int32, (SUP, K), 1)
        row3 = lax.broadcasted_iota(jnp.int32, (SUP, K), 0) + start
        block = jnp.where((lane3 < sup_end) & (lane3 > row3), 0.0, block)
        w[rest, :] = old - mm(left, block)
    return corner


def factor_both(wg, ws, ug, us):
    for k in range(K // BLK):
        cg = factor_step(wg, ug, k)
        factor_step(ws, us, k)
        off = k * BLK
        tile = off // 128 * 128
        rows = slice(off, off + BLK)
        turned = cg.T[off - tile : off - tile + BLK]
        ug[rows, off:off + BLK] = turned


NZ, NX, NC, NY = 8, 4, 2, 4
CHUNK = 512
SUMS = L + K
PART_A = SUMS // NY
PART_B = PART_A // NX
PIECE = K // NX
BLOCK = PIECE + PART_B + 8


def split(v):
    high = v.astype(jnp.bfloat16)
    return high, (v - high.astype(jnp.float32)).astype(jnp.bfloat16)


def mul(a, b, dims=((1,), (0,))):
    return lax.dot_general(a, b, (dims, ((), ())), preferred_element_type=jnp.float32)


def mul3(a, b, dims=((1,), (0,))):
    ah, al = split(a)
    bh, bl = split(b)
    return mul(ah, bh, dims) + (mul(ah, bl, dims) + mul(al, bh, dims))


def signed_sum(table, v):
    high = v.astype(jnp.bfloat16)
    rest = v - high.astype(jnp.float32)
    mid = rest.astype(jnp.bfloat16)
    low = (rest - mid.astype(jnp.float32)).astype(jnp.bfloat16)
    return mul(table, high) + (mul(table, mid) + mul(table, low))


def table_of(bucket, sign):
    level = lax.broadcasted_iota(jnp.int32, (L, bucket.shape[1]), 0).astype(jnp.float32)
    return jnp.where(level == bucket, 2.0 * sign - 1.0, 0.0).astype(jnp.bfloat16)


def sums_kernel(slab, omega, y_prev, prev_bs, slab_bs, out, slab_v, omega_v, stack, part, got_a, got_b, got_s,
                got_c, got_z, mid_p, mid_a, mid_s, load_sem, a_sem, b_sem, s_sem, c_sem, z_sem, d_sem, e_sem, f_sem, g_sem):
    z, x, c, y = (lax.axis_index(name) for name in ("z", "x", "core", "y"))

    def at(dz=0, dx=0, dc=0, dy=0):
        return {"z": (z + dz) % NZ, "x": (x + dx) % NX, "core": (c + dc) % NC, "y": (y + dy) % NY}

    def send(src, dst, sems, i, where):
        copy = pltpu.make_async_remote_copy(
            src_ref=src, dst_ref=dst, send_sem=sems.at[0, i], recv_sem=sems.at[1, i], device_id=where, device_id_type=MESH
        )
        copy.start()
        return copy

    barrier = pltpu.get_barrier_semaphore()
    peers = [at(dz=d) for d in range(1, NZ)]
    peers += [at(dy=d, dc=e) for d in range(NY) for e in range(NC) if d or e]
    peers += [at(dx=d, dc=e) for d in range(1, NX) for e in range(NC)]
    for peer in peers:
        pl.semaphore_signal(barrier, inc=1, device_id=peer, device_id_type=MESH)

    chunks = slab_v.shape[0]
    loads = []
    for i in range(chunks):
        loads.append(pltpu.make_async_copy(slab.at[:, pl.ds(i * CHUNK, CHUNK)], slab_v.at[i], load_sem.at[0, i]))
        loads.append(pltpu.make_async_copy(omega.at[pl.ds(i * CHUNK, CHUNK), :], omega_v.at[i], load_sem.at[1, i]))
    for load in loads:
        load.start()

    table = jnp.concatenate([table_of(prev_bs[h : h + 1, :], prev_bs[h + 2 : h + 3, :]) for h in (0, 1)], axis=1)
    own = y_prev[...]
    stack[:L, :] = signed_sum(table, own)
    stack[L:, :] = mm(own, own, ((0,), (0,)))
    out[c, y, x, PIECE + PART_B :, :] = slab_bs[...]

    pl.semaphore_wait(barrier, len(peers))

    group = [(d, e) for d in range(NY) for e in range(NC) if d or e]
    sent_a = []
    for i, (d, e) in enumerate(group):
        where = at(dy=d, dc=e)
        piece = stack.at[pl.ds(pl.multiple_of(where["y"] * PART_A, 8), PART_A), pl.ds(pl.multiple_of(where["core"] * 128, 128), 128)]
        sent_a.append(send(piece, got_a.at[i], a_sem, i, where))

    part[...] = jnp.zeros_like(part)

    @pl.loop(0, chunks)
    def _(i):
        pltpu.make_async_copy(slab.at[:, pl.ds(0, CHUNK)], slab_v.at[i], load_sem.at[0, i]).wait()
        pltpu.make_async_copy(omega.at[pl.ds(0, CHUNK), :], omega_v.at[i], load_sem.at[1, i]).wait()
        part[...] += mul3(slab_v[i], omega_v[i])

    sent_b = []
    for i, (d, e) in enumerate(group):
        where = at(dx=d, dc=e)
        piece = part.at[pl.ds(pl.multiple_of(where["x"] * PIECE, 8), PIECE), pl.ds(pl.multiple_of(where["core"] * 128, 128), 128)]
        sent_b.append(send(piece, got_b.at[i], b_sem, i, where))

    for copy in sent_a:
        copy.wait_recv()
    total = stack[pl.ds(pl.multiple_of(y * PART_A, 8), PART_A), pl.ds(pl.multiple_of(c * 128, 128), 128)]
    for i in range(len(group)):
        total = total + got_a[i]
    mid_a[...] = total
    sent_s = []
    for d in range(1, NX):
        where = at(dx=d)
        piece = mid_a.at[pl.ds(pl.multiple_of(where["x"] * PART_B, 8), PART_B), :]
        sent_s.append(send(piece, got_s.at[d - 1], s_sem, d - 1, where))

    for copy in sent_b:
        copy.wait_recv()
    total = part[pl.ds(pl.multiple_of(x * PIECE, 8), PIECE), pl.ds(pl.multiple_of(c * 128, 128), 128)]
    for i in range(len(group)):
        total = total + got_b[i]
    mid_p[...] = total
    sent_c = []
    for d in range(1, NZ):
        where = at(dz=d)
        piece = mid_p.at[pl.ds(pl.multiple_of(where["z"] * 8, 8), 8), :]
        sent_c.append(send(piece, got_c.at[d - 1], c_sem, d - 1, where))

    for copy in sent_s:
        copy.wait_recv()
    total = mid_a[pl.ds(pl.multiple_of(x * PART_B, 8), PART_B), :]
    for d in range(1, NX):
        total = total + got_s[d - 1]
    mid_s[...] = total
    sent_z = [send(mid_s, got_z.at[d - 1], z_sem, d - 1, at(dz=d)) for d in range(1, NZ)]

    for copy in sent_c:
        copy.wait_recv()
    total = mid_p[pl.ds(pl.multiple_of(z * 8, 8), 8), :]
    for d in range(1, NZ):
        total = total + got_c[d - 1]
    tile = pl.ds(pl.multiple_of(z * 8, 8), 8)
    out[c, y, x, tile, :] = total
    sent_d = [send(out.at[c, y, x, tile, :], out.at[c, y, x, tile, :], d_sem, d - 1, at(dz=d)) for d in range(1, NZ)]

    for copy in sent_z:
        copy.wait_recv()
    total = mid_s[...]
    for d in range(1, NZ):
        total = total + got_z[d - 1]
    out[c, y, x, PIECE : PIECE + PART_B, :] = total
    for copy in sent_d:
        copy.wait_recv()

    def first(d):
        return at(dx=d * (1 - c), dy=d * c)

    def second(d):
        return at(dx=d * c, dy=d * (1 - c))

    def spread(block, n, along_first):
        copies = []
        if along_first:
            copies += [send(block, block, e_sem, d - 1, first(d)) for d in range(1, 4)]
        if n < 4:
            copies += [send(block, block, f_sem, 3 * n + d - 1, second(d)) for d in range(1, 4)]
        copies.append(send(block, block, g_sem, n, at(dc=1)))
        return copies

    own_block = out.at[c, y, x]
    sent = spread(own_block, 0, True)
    sent_e, sent_f, sent_g = sent[:3], sent[3:6], sent[6:]
    for d in range(1, 4):
        sent_e[d - 1].wait_recv()
        block = out.at[c, (y + (4 - d) * c) % NY, (x + (4 - d) * (1 - c)) % NX]
        more = spread(block, d, False)
        sent_f += more[:3]
        sent_g += more[3:]
    for n in range(4):
        for d in range(1, 4):
            sent_f[3 * n + d - 1].wait_recv()
            by = (y + (4 - n) * c + (4 - d) * (1 - c)) % NY
            bx = (x + (4 - n) * (1 - c) + (4 - d) * c) % NX
            sent_g += spread(out.at[c, by, bx], 4 + 3 * n + d - 1, False)
    for copy in sent_g:
        copy.wait_recv()
    for copy in sent_a + sent_b + sent_s + sent_c + sent_z + sent_d + sent_e + sent_f + sent_g:
        copy.wait_send()


def sums(slab, omega, y_prev, prev_bs, slab_bs):
    rows, cols = slab.shape
    chunks = cols // CHUNK
    vmem = pl.BlockSpec(memory_space=pltpu.VMEM)
    hbm = pl.BlockSpec(memory_space=pl.ANY)
    f32 = jnp.float32
    dma = pltpu.SemaphoreType.DMA
    return pl.pallas_call(
        sums_kernel,
        out_shape=jax.ShapeDtypeStruct((NC, NY, NX, BLOCK, 128), f32),
        in_specs=[hbm, hbm, vmem, vmem, vmem],
        out_specs=vmem,
        scratch_shapes=[
            pltpu.VMEM((chunks, rows, CHUNK), f32),
            pltpu.VMEM((chunks, CHUNK, K), f32),
            pltpu.VMEM((SUMS, K), f32),
            pltpu.VMEM((rows, K), f32),
            pltpu.VMEM((7, PART_A, 128), f32),
            pltpu.VMEM((7, PIECE, 128), f32),
            pltpu.VMEM((3, PART_B, 128), f32),
            pltpu.VMEM((7, 8, 128), f32),
            pltpu.VMEM((7, PART_B, 128), f32),
            pltpu.VMEM((PIECE, 128), f32),
            pltpu.VMEM((PART_A, 128), f32),
            pltpu.VMEM((PART_B, 128), f32),
            dma((2, chunks)),
            dma((2, 7)),
            dma((2, 7)),
            dma((2, 3)),
            dma((2, 7)),
            dma((2, 7)),
            dma((2, 7)),
            dma((2, 3)),
            dma((2, 12)),
            dma((2, 16)),
        ],
        compiler_params=pltpu.CompilerParams(collective_id=0, has_side_effects=True, vmem_limit_bytes=40 * 2**20),
        cost_estimate=pl.CostEstimate(flops=60_000_000_000, bytes_accessed=10_000_000, transcendentals=0),
        name="sums",
    )(slab, omega, y_prev, prev_bs, slab_bs)


def factors_kernel(place, gathered, y_prev, q_prev, q_new, combined, xg, xs, u, us, ys, zs, ts, mapping):
    for c in range(NC):
        lanes = slice(128 * c, 128 * c + 128)
        for y in range(NY):
            for x in range(NX):
                ys[pl.ds(256 * y + PIECE * x, PIECE), lanes] = gathered[c, y, x, :PIECE, :]
                zs[pl.ds(PART_A * y + PART_B * x, PART_B), lanes] = gathered[c, y, x, PIECE : PIECE + PART_B, :]
    for y in range(NY):
        bs = gathered[0, y, 0, PIECE + PART_B :, :]
        for h in (0, 1):
            ts[:, 256 * y + 128 * h : 256 * y + 128 * h + 128] = table_of(bs[h : h + 1], bs[h + 2 : h + 3])
    new = ys[...]
    xg[...] = zs[L:, :] + mm(new, new, ((0,), (0,)))
    zs[:L, :] = zs[:L, :] + signed_sum(ts[...], new)
    sketch = zs[:L, :]
    xs[...] = mm(sketch, sketch, ((0,), (0,)))
    factor_both(xg, xs, u, us)
    row = lax.broadcasted_iota(jnp.int32, (K, K), 0)
    lane = lax.broadcasted_iota(jnp.int32, (K, K), 1)
    outer = jnp.where(lane <= row, xg[...], 0.0)
    inner = jnp.where(lane <= row, xs[...], 0.0)
    core = mm(mm(u[...], inner, ((1,), (1,))), inner)
    found = mm(core, zs[:L, :], ((1,), (1,)))
    mapping[...] = found
    y_place = place[0]
    cols = pl.ds(pl.multiple_of(y_place * 256, 256), 256)
    table = ts[:, cols]
    high = found.astype(jnp.bfloat16)
    rest = found - high.astype(jnp.float32)
    mid = rest.astype(jnp.bfloat16)
    low = (rest - mid.astype(jnp.float32)).astype(jnp.bfloat16)
    combined[:, :256] = mul(high, table) + (mul(mid, table) + mul(low, table))
    combined[:, 256:] = mapping[:, pl.ds(pl.multiple_of(y_place * 128, 128), 128)]
    q_prev[...] = mm(y_prev[...], outer, ((1,), (1,)))
    q_new[...] = mm(ys[pl.ds(pl.multiple_of(place[1] * 8, 8), 8), :], outer, ((1,), (1,)))


def factors(place, gathered, y_prev):
    vmem = pl.BlockSpec(memory_space=pltpu.VMEM)
    f32 = jnp.float32
    return pl.pallas_call(
        factors_kernel,
        out_shape=(
            jax.ShapeDtypeStruct(y_prev.shape, f32),
            jax.ShapeDtypeStruct((8, K), f32),
            jax.ShapeDtypeStruct((K, 384), f32),
        ),
        in_specs=[pl.BlockSpec(memory_space=pltpu.SMEM), vmem, vmem],
        out_specs=[vmem] * 3,
        scratch_shapes=[pltpu.VMEM((K, K), f32)] * 4
        + [pltpu.VMEM((1024, K), f32), pltpu.VMEM((SUMS, K), f32), pltpu.VMEM((L, 1024), jnp.bfloat16), pltpu.VMEM((K, L), f32)],
        compiler_params=pltpu.CompilerParams(vmem_limit_bytes=40 * 2**20),
        cost_estimate=pl.CostEstimate(flops=20_000_000_000, bytes_accessed=3_000_000, transcendentals=0),
        name="factors",
    )(place, gathered, y_prev)


def in_blocks(x, dim, size):
    before, after = (x.shape[:dim], x.shape[dim + 1 :])
    return jnp.moveaxis(x.reshape(*before, size, -1, *after), dim, 0)


def sum_at_owner(x, axis, dim):
    size = lax.axis_size(axis)
    blocks = lax.all_to_all(in_blocks(x, dim, size), axis, 0, 0, tiled=True)
    return jnp.sum(blocks, axis=0)


def matmul(left, right):
    return jnp.dot(left, right, precision=highest, preferred_element_type=jnp.float32)


def as_rows(bucket, sign):
    rows = jnp.concatenate([bucket.reshape(2, 128), sign.reshape(2, 128)]).astype(jnp.float32)
    return jnp.concatenate([rows, jnp.zeros((4, 128), jnp.float32)])


def on_device(slab, omega, y_prev, w_prev, prev_bucket, prev_sign, slab_bucket, slab_sign):
    y = lax.axis_index("y")
    col = lax.axis_index(COL)
    gathered = sums(slab, omega, y_prev, as_rows(prev_bucket, prev_sign), as_rows(slab_bucket, slab_sign))
    place = jnp.stack([y, y * 32 + col // 2]).astype(jnp.int32)
    q_prev, q_pair, combined = factors(place, gathered, y_prev)
    q_new = lax.dynamic_slice_in_dim(q_pair, (col % 2) * 4, 4, 0)
    first = matmul(combined[:, :256], slab)
    x_core = sum_at_owner(first + matmul(combined[:, 256:], w_prev), "y", 0)
    return (q_prev, q_new, x_core)


def solution(mesh):
    finer = Mesh(mesh.devices.reshape(NZ, NX, NC, NY), ("z", "x", "core", "y"))
    return jax.shard_map(
        on_device,
        mesh=finer,
        in_specs=(
            P("y", COL),
            P(COL, None),
            P(ROW_COL, None),
            P("y", COL),
            P(ROW_COL),
            P(ROW_COL),
            P("y"),
            P("y"),
        ),
        out_specs=(P(ROW_COL, None), P(ROW_COL, None), P("y", COL)),
        check_vma=False,
    )
```

time: 195 us -> 137 us (0.70)
  blocking collectives: 50.7 us -> 0 us
  Pallas kernels: 14.2 us -> 62.7 us
  waiting for transfers between devices: 68.2 us -> 48.3 us
  starting transfers between devices: 20.6 us -> 4.84 us
  matrix products: 22.7 us -> 8.94 us
  local copies, waits for them, and re-layouts: 11.9 us -> 5.95 us
    all_to_all x4 -> x0, blocking collectives: 50.7 us -> none  [the longest x2 25.3 us: sum_at_owner(): blocks = lax.all_to_all(in_blocks(x, dim, size), axis, 0, 0, tiled=True)]
    pallas_call x1 -> x2, Pallas kernels: 14.2 us -> 62.7 us  [the longest x1 46.3 us: sums(): pl.pallas_call(sums_kernel, out_shape=jax.ShapeDtypeStruct((NC, NY, NX, B...]
    all_to_all x2 -> x0, waiting for transfers between devices: 21.3 us -> none  [the longest x1 12.2 us: from_everyone(): return lax.all_to_all(copies, axis, split_axis=0, concat_axis=0, tiled=True)]
    all_to_all x2 -> x0, starting transfers between devices: 15.7 us -> none  [the longest x1 9.33 us: sum_in_two_steps(): lax.all_to_all(nearer, far, split_axis=0, concat_axis=0, tiled=True)]
    dot_general x7 -> x2, matrix products: 22.7 us -> 8.94 us  [matmul(): jnp.dot(left, right, precision=highest, preferred_element_type=jnp.float32)]
    slice x4 -> x0, local copies, waits for them, and re-layouts: 4.84 us -> none  [the longest x2 3.52 us: on_device(): inverse, mapping = factors(both[L:], both[:L])]
    unnamed x16 -> x10, local copies, waits for them, and re-layouts: 0.91 us -> 5.34 us
    another operation x4 -> x0, local copies, waits for them, and re-layouts: 2.83 us -> none  [the longest x3 1.56 us: in_blocks(): return jnp.moveaxis(x.reshape(*before, size, -1, *after), dim, 0)]
  transfers between devices with their start and end apart: 3 -> 1, of which waited for: 3 -> 1; matrix products, arithmetic and copies ran while one was open for 1% -> 0% of each run, Pallas kernels for 0% -> 0%
where the time goes in v1:
time: 137 us
  Pallas kernels  62.7 us (46%)
  waiting for transfers between devices  48.3 us (35%)
  matrix products  8.94 us (7%)
  local copies, waits for them, and re-layouts  5.95 us (4%)
  other arithmetic  5.13 us (4%)
  starting transfers between devices  4.84 us (4%)
    all_to_all x1, waiting for transfers between devices, sum_at_owner(): blocks = lax.all_to_all(in_blocks(x, dim, size), axis, 0, 0, tiled=True)  48.3 us
    pallas_call x1, Pallas kernels, sums(): pl.pallas_call(sums_kernel, out_shape=jax.ShapeDtypeStruct((NC, NY, NX, B...  46.3 us
    pallas_call x1, Pallas kernels, factors(): pl.pallas_call(factors_kernel, out_shape=(jax.ShapeDtypeStruct(y_prev.sha...  16.3 us
    dot_general x2, matrix products, matmul(): jnp.dot(left, right, precision=highest, preferred_element_type=jnp.float32)  8.94 us
    unnamed x10, local copies, waits for them, and re-layouts  5.34 us
    all_to_all x1, starting transfers between devices, sum_at_owner(): blocks = lax.all_to_all(in_blocks(x, dim, size), axis, 0, 0, tiled=True)  4.84 us
    reduce_sum x1, other arithmetic, sum_at_owner(): return jnp.sum(blocks, axis=0)  3.5 us
  transfers between devices with their start and end apart: 1, of which 1 were waited for; matrix products, arithmetic and copies ran while one was open for 0% of the time, Pallas kernels for 0%

profile of v1, /device:TPU:1, one launch (start us, length us, event | category | flops | bytes accessed | tf_op | source)
XLA Modules:
  0.0 136.6 jit_solution(10888072326630794374)
XLA Ops:
  0.6 0.0 copy-start
  0.7 0.8 add_convert_fusion
  1.5 0.7 add_convert_fusion.1
  2.2 0.1 pad_add_fusion.place
  2.3 0.0 copy-start.1
  2.3 2.2 %copy-done.1 = f32[256,4096]{1,0:T(8,128)S(1)} copy-done((f32[256,4096]{1,0:T(8,128)S(1)}, f32[256,4096]{1,0:T(8,128)}, u32[]{:S(2)}) %copy-start.1) | copy-done | bytes 4194328
  4.5 0.0 copy-start.3
  4.5 2.2 %copy-done.3 = f32[4096,256]{1,0:T(8,128)S(1)} copy-done((f32[4096,256]{1,0:T(8,128)S(1)}, f32[4096,256]{1,0:T(8,128)}, u32[]{:S(2)}) %copy-start.3) | copy-done | bytes 4194328
  6.7 0.0 copy-start.4
  6.7 0.9 copy-done.4
  7.6 46.3 %sums.1.gathered = f32[2,4,4,120,128]{4,3,2,1,0:T(8,128)S(1)} custom-call(f32[256,4096]{1,0:T(8,128)S(1)} %copy-done.1, f32[4096,256]{1,0:T(8,128)S(1)} %copy-done.3, f32[256,256]{1,0:T(8,128)S(1)} %copy-done.4, f32[8,128]{1,0:T(8,128)S(1)} %concatenate.13.prev_bs, f32[8,128]{1,0:T(8,128)S(1)} %concatenate.15.slab_bs), custom_call_target="tpu_custom_call" | custom-call | flops 60000002048 | bytes 10000000 | tf_op jit(solution)/shard_map/sums/pallas_call | solution.py:313
  54.0 0.0 copy-start.2
  54.0 16.3 %factors.1 = (f32[256,256]{1,0:T(8,128)}, f32[8,256]{1,0:T(8,128)S(1)}, f32[256,384]{1,0:T(8,128)S(1)}) custom-call(s32[2]{0:T(128)S(1)} %pad_add_fusion.place, f32[2,4,4,120,128]{4,3,2,1,0:T(8,128)S(1)} %sums.1.gathered, f32[256,256]{1,0:T(8,128)S(1)} %copy-done.4), custom_call_target="tpu_custom_call" | custom-call | flops 20000000000 | bytes 3000000 | tf_op jit(solution)/shard_map/factors/pallas_call | solution.py:388
  70.3 0.0 copy-done.2
  70.3 3.9 %fusion = f32[256,4096]{1,0:T(8,128)S(1)} fusion(f32[256,4096]{1,0:T(8,128)S(1)} %copy-done.2, f32[256,384]{1,0:T(8,128)S(1)} %get-tuple-element.8), kind=kOutput, calls=%fused_computation.1 | convolution fusion | flops 3221225472 | bytes 8650752 | tf_op jit(solution)/shard_map/dot_general | solution.py:417
  74.3 0.0 copy-done
  74.3 5.0 %convolution_add_fusion = f32[256,4096]{1,0:T(8,128)} fusion(f32[256,4096]{1,0:T(8,128)S(1)} %fusion, f32[128,4096]{1,0:T(8,128)S(1)} %copy-done, f32[256,384]{1,0:T(8,128)S(1)} %get-tuple-element.8), kind=kOutput, calls=%fused_computation | convolution fusion | flops 1611661312 | bytes 10616832 | tf_op jit(solution)/shard_map/dot_general | solution.py:417
  79.3 4.8 %all-to-all-start = ((f32[4,64,4096]{2,1,0:T(8,128)}), f32[4,64,4096]{2,1,0:T(8,128)}, u32[]{:S(2)}, u32[]{:S(2)}) async-start(f32[4,64,4096]{2,1,0:T(8,128)} %bitcast.9), calls=%async_computation | async-start | bytes 8388608 | tf_op jit(solution)/shard_map/all_to_all | solution.py:412
  84.1 0.6 constant_dynamic-slice_fusion
  84.8 48.3 %all-to-all-done = f32[4,64,4096]{2,1,0:T(8,128)} async-done(((f32[4,64,4096]{2,1,0:T(8,128)}), f32[4,64,4096]{2,1,0:T(8,128)}, u32[]{:S(2)}, u32[]{:S(2)}) %all-to-all-start) | async-done | bytes 4194336 | tf_op jit(solution)/shard_map/all_to_all | solution.py:412
  133.1 3.5 %reduce_sum.9 = f32[64,4096]{1,0:T(8,128)} reduce(f32[4,64,4096]{2,1,0:T(8,128)} %all-to-all-done, f32[]{:T(128)} %constant.49.clone.1), dimensions={0}, to_apply=%region_0.1 | reduce | flops 786432 | bytes 5242884 | tf_op jit(solution)/shard_map/reduce_sum | solution.py:413
  (2 shorter events, 0.0 us)
Async XLA Ops:
  0.6 73.6 %copy-start = (f32[128,4096]{1,0:T(8,128)S(1)}, f32[128,4096]{1,0:T(8,128)}, u32[]{:S(2)}) copy-start(f32[128,4096]{1,0:T(8,128)} %param.11) | copy-start | bytes 6291460
  2.3 2.2 %copy-start.1 = (f32[256,4096]{1,0:T(8,128)S(1)}, f32[256,4096]{1,0:T(8,128)}, u32[]{:S(2)}) copy-start(f32[256,4096]{1,0:T(8,128)} %slab.1) | copy-start | bytes 12582916
  4.5 2.2 %copy-start.3 = (f32[4096,256]{1,0:T(8,128)S(1)}, f32[4096,256]{1,0:T(8,128)}, u32[]{:S(2)}) copy-start(f32[4096,256]{1,0:T(8,128)} %omega.1) | copy-start | bytes 12582916
  6.7 0.9 copy-start.4
  54.0 16.3 %copy-start.2 = (f32[256,4096]{1,0:T(8,128)S(1)}, f32[256,4096]{1,0:T(8,128)}, u32[]{:S(2)}) copy-start(f32[256,4096]{1,0:T(8,128)} %slab.1) | copy-start | bytes 12582916
  79.3 53.8 %all-to-all-start = ((f32[4,64,4096]{2,1,0:T(8,128)}), f32[4,64,4096]{2,1,0:T(8,128)}, u32[]{:S(2)}, u32[]{:S(2)}) async-start(f32[4,64,4096]{2,1,0:T(8,128)} %bitcast.9), calls=%async_computation | async-start | bytes 8388608 | tf_op jit(solution)/shard_map/all_to_all | solution.py:412

commit v2 on v1

--- a/solution.py
+++ b/solution.py
@@ -1,5 +1,3 @@
-import functools
-
 import jax
 import jax.numpy as jnp
 from jax import lax
@@ -307,7 +305,7 @@
     rows, cols = slab.shape
     chunks = cols // CHUNK
     vmem = pl.BlockSpec(memory_space=pltpu.VMEM)
-    hbm = pl.BlockSpec(memory_space=pl.ANY)
+    hbm = pl.BlockSpec(memory_space=pltpu.HBM)
     f32 = jnp.float32
     dma = pltpu.SemaphoreType.DMA
     return pl.pallas_call(
@@ -339,7 +337,7 @@
             dma((2, 12)),
             dma((2, 16)),
         ],
-        compiler_params=pltpu.CompilerParams(collective_id=0, has_side_effects=True, vmem_limit_bytes=40 * 2**20),
+        compiler_params=pltpu.CompilerParams(collective_id=0, has_side_effects=True, vmem_limit_bytes=63_500_000),
         cost_estimate=pl.CostEstimate(flops=60_000_000_000, bytes_accessed=10_000_000, transcendentals=0),
         name="sums",
     )(slab, omega, y_prev, prev_bs, slab_bs)
@@ -402,19 +400,88 @@
     )(place, gathered, y_prev)
 
 
-def in_blocks(x, dim, size):
-    before, after = (x.shape[:dim], x.shape[dim + 1 :])
-    return jnp.moveaxis(x.reshape(*before, size, -1, *after), dim, 0)
-
-
-def sum_at_owner(x, axis, dim):
-    size = lax.axis_size(axis)
-    blocks = lax.all_to_all(in_blocks(x, dim, size), axis, 0, 0, tiled=True)
-    return jnp.sum(blocks, axis=0)
-
-
-def matmul(left, right):
-    return jnp.dot(left, right, precision=highest, preferred_element_type=jnp.float32)
+def core_kernel(combined, slab, w_prev, out, terms, far_l, far_r, near_l, near_r, far_sem, near_sem):
+    y = lax.axis_index("y")
+    chunks = terms.shape[0]
+    half = chunks // 2
+    rows = out.shape[0]
+    up, down, across = (y + 1) % NY, (y + 3) % NY, (y + 2) % NY
+
+    barrier = pltpu.get_barrier_semaphore()
+    for peer in (up, down):
+        pl.semaphore_signal(barrier, inc=1, device_id={"y": peer}, device_id_type=MESH)
+    order = [n for i in range(half) for n in (i, half + i)]
+
+    def block(n, place):
+        return terms.at[n, pl.ds(pl.multiple_of(place * rows, 8), rows), :]
+
+    def send(src, dst, send_sem, recv_sem, peer):
+        return pltpu.make_async_remote_copy(
+            src_ref=src, dst_ref=dst, send_sem=send_sem, recv_sem=recv_sem, device_id={"y": peer}, device_id_type=MESH
+        )
+
+    far = [
+        send(block(n, across), far_l.at[n], far_sem.at[0, n], far_sem.at[1, n], up)
+        if n < half
+        else send(block(n, across), far_r.at[n - half], far_sem.at[0, n], far_sem.at[1, n], down)
+        for n in range(chunks)
+    ]
+    to_up = [send(block(n, up), near_l.at[n], near_sem.at[0, n], near_sem.at[1, n], up) for n in range(chunks)]
+    to_down = [send(block(n, down), near_r.at[n], near_sem.at[2, n], near_sem.at[3, n], down) for n in range(chunks)]
+
+    for i, n in enumerate(order):
+        cols = slice(n * CHUNK, n * CHUNK + CHUNK)
+        terms[n] = mul3(combined[...], jnp.concatenate([slab[:, cols], w_prev[:, cols]], axis=0))
+        if i == 0:
+            pl.semaphore_wait(barrier, 2)
+        far[n].start()
+    for i in range(half):
+        to_up[half + i].start()
+        to_down[i].start()
+    for i in range(half):
+        far[i].wait_recv()
+        spot = pl.ds(pl.multiple_of(up * rows, 8), rows)
+        terms[i, spot, :] = terms[i, spot, :] + far_l[i]
+        to_up[i].start()
+        far[half + i].wait_recv()
+        spot = pl.ds(pl.multiple_of(down * rows, 8), rows)
+        terms[half + i, spot, :] = terms[half + i, spot, :] + far_r[i]
+        to_down[half + i].start()
+    own = pl.ds(pl.multiple_of(y * rows, 8), rows)
+    for i in range(half):
+        for n in (i, half + i):
+            to_up[n].wait_recv()
+            to_down[n].wait_recv()
+            out[:, n * CHUNK : n * CHUNK + CHUNK] = terms[n, own, :] + (near_l[n] + near_r[n])
+    for copy in far + to_up + to_down:
+        copy.wait_send()
+
+
+def core_product(combined, slab, w_prev):
+    cols = slab.shape[1]
+    chunks = cols // CHUNK
+    rows = K // NY
+    vmem = pl.BlockSpec(memory_space=pltpu.VMEM)
+    f32 = jnp.float32
+    dma = pltpu.SemaphoreType.DMA
+    return pl.pallas_call(
+        core_kernel,
+        out_shape=jax.ShapeDtypeStruct((rows, cols), f32),
+        in_specs=[vmem, vmem, vmem],
+        out_specs=vmem,
+        scratch_shapes=[
+            pltpu.VMEM((chunks, K, CHUNK), f32),
+            pltpu.VMEM((chunks // 2, rows, CHUNK), f32),
+            pltpu.VMEM((chunks // 2, rows, CHUNK), f32),
+            pltpu.VMEM((chunks, rows, CHUNK), f32),
+            pltpu.VMEM((chunks, rows, CHUNK), f32),
+            dma((2, chunks)),
+            dma((4, chunks)),
+        ],
+        compiler_params=pltpu.CompilerParams(collective_id=1, has_side_effects=True, vmem_limit_bytes=40 * 2**20),
+        cost_estimate=pl.CostEstimate(flops=60_000_000_000, bytes_accessed=10_000_000, transcendentals=0),
+        name="core_product",
+    )(combined, slab, w_prev)
 
 
 def as_rows(bucket, sign):
@@ -429,8 +496,7 @@
     place = jnp.stack([y, y * 32 + col // 2]).astype(jnp.int32)
     q_prev, q_pair, combined = factors(place, gathered, y_prev)
     q_new = lax.dynamic_slice_in_dim(q_pair, (col % 2) * 4, 4, 0)
-    first = matmul(combined[:, :256], slab)
-    x_core = sum_at_owner(first + matmul(combined[:, 256:], w_prev), "y", 0)
+    x_core = core_product(combined, slab, w_prev)
     return (q_prev, q_new, x_core)
 
 

time: 137 us -> 109 us (0.80)
  waiting for transfers between devices: 48.3 us -> 0 us
  Pallas kernels: 62.7 us -> 103 us
  matrix products: 8.94 us -> 0 us
  starting transfers between devices: 4.84 us -> 0 us
  other arithmetic: 5.13 us -> 1.49 us
  local copies, waits for them, and re-layouts: 5.95 us -> 4.31 us
    all_to_all x1 -> x0, waiting for transfers between devices: 48.3 us -> none  [sum_at_owner(): blocks = lax.all_to_all(in_blocks(x, dim, size), axis, 0, 0, tiled=True)]
    pallas_call x0 -> x1, Pallas kernels: none -> 37.6 us  [core_product(): pl.pallas_call(core_kernel, out_shape=jax.ShapeDtypeStruct((rows, cols),...]
    dot_general x2 -> x0, matrix products: 8.94 us -> none  [matmul(): jnp.dot(left, right, precision=highest, preferred_element_type=jnp.float32)]
    all_to_all x1 -> x0, starting transfers between devices: 4.84 us -> none  [sum_at_owner(): blocks = lax.all_to_all(in_blocks(x, dim, size), axis, 0, 0, tiled=True)]
    reduce_sum x1 -> x0, other arithmetic: 3.5 us -> none  [sum_at_owner(): return jnp.sum(blocks, axis=0)]
    unnamed x10 -> x9, local copies, waits for them, and re-layouts: 5.34 us -> 2.52 us
    pallas_call x1, Pallas kernels: 46.3 us -> 48.7 us  [sums(): pl.pallas_call(sums_kernel, out_shape=jax.ShapeDtypeStruct((NC, NY, NX, B...]
  transfers between devices with their start and end apart: 1 -> 0, of which waited for: 1 -> 0; matrix products, arithmetic and copies ran while one was open for 0% -> 0% of each run, Pallas kernels for 0% -> 0%
where the time goes in v2:
time: 109 us
  Pallas kernels  103 us (94%)
  local copies, waits for them, and re-layouts  4.31 us (4%)
  other arithmetic  1.49 us (1%)
    pallas_call x1, Pallas kernels, sums(): pl.pallas_call(sums_kernel, out_shape=jax.ShapeDtypeStruct((NC, NY, NX, B...  48.7 us
    pallas_call x1, Pallas kernels, core_product(): pl.pallas_call(core_kernel, out_shape=jax.ShapeDtypeStruct((rows, cols),...  37.6 us
    pallas_call x1, Pallas kernels, factors(): pl.pallas_call(factors_kernel, out_shape=(jax.ShapeDtypeStruct(y_prev.sha...  16.3 us
    unnamed x9, local copies, waits for them, and re-layouts  2.52 us

profile of v2, /device:TPU:1, one launch (start us, length us, event | category | flops | bytes accessed | tf_op | source)
XLA Modules:
  0.0 109.1 jit_solution(17880644844100753031)
XLA Ops:
  0.7 0.1 pad_add_fusion.place
  0.7 0.7 add_convert_fusion
  1.4 0.6 concatenate.13.prev_bs
  2.0 0.7 add_convert_fusion.1
  2.8 0.6 concatenate.15.slab_bs
  3.3 0.0 copy-start.2
  3.4 48.7 %sums.1.gathered = f32[2,4,4,120,128]{4,3,2,1,0:T(8,128)} custom-call(f32[256,4096]{1,0:T(8,128)} %slab.3, f32[4096,256]{1,0:T(8,128)} %omega.1, f32[256,256]{1,0:T(8,128)} %y_prev.3, f32[8,128]{1,0:T(8,128)} %concatenate.13.prev_bs, f32[8,128]{1,0:T(8,128)} %concatenate.15.slab_bs), custom_call_target="tpu_custom_call" | custom-call | flops 60000002048 | bytes 10000000 | tf_op jit(solution)/shard_map/sums/pallas_call | solution.py:311
  52.0 0.0 copy-done.2
  52.0 0.0 copy-start.3
  52.0 1.5 %copy-done.3 = f32[2,4,4,120,128]{4,3,2,1,0:T(8,128)S(1)} copy-done((f32[2,4,4,120,128]{4,3,2,1,0:T(8,128)S(1)}, f32[2,4,4,120,128]{4,3,2,1,0:T(8,128)}, u32[]{:S(2)}) %copy-start.3) | copy-done | bytes 1966104
  53.6 0.0 copy-start
  53.6 0.0 copy-start.1
  53.6 16.3 %factors.1 = (f32[256,256]{1,0:T(8,128)}, f32[8,256]{1,0:T(8,128)S(1)}, f32[256,384]{1,0:T(8,128)S(1)}) custom-call(s32[2]{0:T(128)S(1)} %pad_add_fusion.place, f32[2,4,4,120,128]{4,3,2,1,0:T(8,128)S(1)} %copy-done.3, f32[256,256]{1,0:T(8,128)S(1)} %copy-done.2), custom_call_target="tpu_custom_call" | custom-call | flops 20000000000 | bytes 3000000 | tf_op jit(solution)/shard_map/factors/pallas_call | solution.py:386
  69.9 0.6 constant_dynamic-slice_fusion
  70.4 0.0 copy-done
  70.5 0.0 copy-done.1
  70.5 37.6 %core_product.1 = f32[64,4096]{1,0:T(8,128)S(1)} custom-call(f32[256,384]{1,0:T(8,128)S(1)} %get-tuple-element.8.combined, f32[256,4096]{1,0:T(8,128)S(1)} %copy-done, f32[128,4096]{1,0:T(8,128)S(1)} %copy-done.1), custom_call_target="tpu_custom_call" | custom-call | flops 60000002048 | bytes 10000000 | tf_op jit(solution)/shard_map/core_product/pallas_call | solution.py:467
  108.1 1.0 copy.12
Async XLA Ops:
  3.3 48.7 %copy-start.2 = (f32[256,256]{1,0:T(8,128)S(1)}, f32[256,256]{1,0:T(8,128)}, u32[]{:S(2)}) copy-start(f32[256,256]{1,0:T(8,128)} %y_prev.3) | copy-start | bytes 786436
  52.0 1.5 %copy-start.3 = (f32[2,4,4,120,128]{4,3,2,1,0:T(8,128)S(1)}, f32[2,4,4,120,128]{4,3,2,1,0:T(8,128)}, u32[]{:S(2)}) copy-start(f32[2,4,4,120,128]{4,3,2,1,0:T(8,128)} %sums.1.gathered) | copy-start | bytes 5898244
  53.6 16.9 %copy-start = (f32[256,4096]{1,0:T(8,128)S(1)}, f32[256,4096]{1,0:T(8,128)}, u32[]{:S(2)}) copy-start(f32[256,4096]{1,0:T(8,128)} %slab.3) | copy-start | bytes 12582916
  53.6 16.9 %copy-start.1 = (f32[128,4096]{1,0:T(8,128)S(1)}, f32[128,4096]{1,0:T(8,128)}, u32[]{:S(2)}) copy-start(f32[128,4096]{1,0:T(8,128)} %w_prev.1) | copy-start | bytes 6291460

commit v3 on v2

--- a/solution.py
+++ b/solution.py
@@ -123,10 +123,10 @@
 NZ, NX, NC, NY = 8, 4, 2, 4
 CHUNK = 512
 SUMS = L + K
-PART_A = SUMS // NY
+PART_A = SUMS // 2 // NY
 PART_B = PART_A // NX
 PIECE = K // NX
-BLOCK = PIECE + PART_B + 8
+BLOCK = PIECE + 2 * PART_B + 8
 
 
 def split(v):
@@ -157,7 +157,7 @@
     return jnp.where(level == bucket, 2.0 * sign - 1.0, 0.0).astype(jnp.bfloat16)
 
 
-def sums_kernel(slab, omega, y_prev, prev_bs, slab_bs, out, slab_v, omega_v, stack, part, got_a, got_b, got_s,
+def sums_kernel(slab, omega, y_prev, prev_bucket, prev_sign, slab_bucket, slab_sign, out, slab_v, omega_v, stack, part, got_a, got_b, got_s,
                 got_c, got_z, mid_p, mid_a, mid_s, load_sem, a_sem, b_sem, s_sem, c_sem, z_sem, d_sem, e_sem, f_sem, g_sem):
     z, x, c, y = (lax.axis_index(name) for name in ("z", "x", "core", "y"))
 
@@ -186,28 +186,41 @@
     for load in loads:
         load.start()
 
-    table = jnp.concatenate([table_of(prev_bs[h : h + 1, :], prev_bs[h + 2 : h + 3, :]) for h in (0, 1)], axis=1)
+    def real(ref):
+        return ref[...].astype(jnp.float32)
+
+    bucket, sign = real(prev_bucket), real(prev_sign)
+    table = jnp.concatenate([table_of(bucket[h : h + 1], sign[h : h + 1]) for h in (0, 1)], axis=1)
     own = y_prev[...]
     stack[:L, :] = signed_sum(table, own)
     stack[L:, :] = mm(own, own, ((0,), (0,)))
-    out[c, y, x, PIECE + PART_B :, :] = slab_bs[...]
-
-    pl.semaphore_wait(barrier, len(peers))
-
-    group = [(d, e) for d in range(NY) for e in range(NC) if d or e]
-    sent_a = []
-    for i, (d, e) in enumerate(group):
-        where = at(dy=d, dc=e)
-        piece = stack.at[pl.ds(pl.multiple_of(where["y"] * PART_A, 8), PART_A), pl.ds(pl.multiple_of(where["core"] * 128, 128), 128)]
-        sent_a.append(send(piece, got_a.at[i], a_sem, i, where))
-
+    out[c, y, x, PIECE + 2 * PART_B :, :] = jnp.concatenate([real(slab_bucket), real(slab_sign), jnp.zeros((4, 128), jnp.float32)])
     part[...] = jnp.zeros_like(part)
 
-    @pl.loop(0, chunks)
-    def _(i):
+    def multiply(i):
         pltpu.make_async_copy(slab.at[:, pl.ds(0, CHUNK)], slab_v.at[i], load_sem.at[0, i]).wait()
         pltpu.make_async_copy(omega.at[pl.ds(0, CHUNK), :], omega_v.at[i], load_sem.at[1, i]).wait()
         part[...] += mul3(slab_v[i], omega_v[i])
+
+    pl.loop(0, 2)(multiply)
+    pl.semaphore_wait(barrier, len(peers))
+
+    group = [(d, e) for d in range(NY) for e in range(NC) if d or e]
+
+    def share(half, where):
+        place = where["x"] if half else where["y"]
+        return (
+            pl.ds(pl.multiple_of(half * (SUMS // 2) + place * PART_A, 8), PART_A),
+            pl.ds(pl.multiple_of(where["core"] * 128, 128), 128),
+        )
+
+    sent_a = []
+    for i, (d, e) in enumerate(group):
+        for half in (0, 1):
+            where = at(dx=d, dc=e) if half else at(dy=d, dc=e)
+            sent_a.append(send(stack.at[share(half, where)], got_a.at[half, i], a_sem, 2 * i + half, where))
+
+    pl.loop(2, chunks)(multiply)
 
     sent_b = []
     for i, (d, e) in enumerate(group):
@@ -217,15 +230,18 @@
 
     for copy in sent_a:
         copy.wait_recv()
-    total = stack[pl.ds(pl.multiple_of(y * PART_A, 8), PART_A), pl.ds(pl.multiple_of(c * 128, 128), 128)]
-    for i in range(len(group)):
-        total = total + got_a[i]
-    mid_a[...] = total
+    for half in (0, 1):
+        total = stack[share(half, at())]
+        for i in range(len(group)):
+            total = total + got_a[half, i]
+        mid_a[half] = total
     sent_s = []
     for d in range(1, NX):
-        where = at(dx=d)
-        piece = mid_a.at[pl.ds(pl.multiple_of(where["x"] * PART_B, 8), PART_B), :]
-        sent_s.append(send(piece, got_s.at[d - 1], s_sem, d - 1, where))
+        for half in (0, 1):
+            where = at(dy=d) if half else at(dx=d)
+            place = where["y"] if half else where["x"]
+            piece = mid_a.at[half, pl.ds(pl.multiple_of(place * PART_B, 8), PART_B), :]
+            sent_s.append(send(piece, got_s.at[half, d - 1], s_sem, 2 * (d - 1) + half, where))
 
     for copy in sent_b:
         copy.wait_recv()
@@ -241,10 +257,11 @@
 
     for copy in sent_s:
         copy.wait_recv()
-    total = mid_a[pl.ds(pl.multiple_of(x * PART_B, 8), PART_B), :]
-    for d in range(1, NX):
-        total = total + got_s[d - 1]
-    mid_s[...] = total
+    for half in (0, 1):
+        total = mid_a[half, pl.ds(pl.multiple_of((y if half else x) * PART_B, 8), PART_B), :]
+        for d in range(1, NX):
+            total = total + got_s[half, d - 1]
+        mid_s[half * PART_B : half * PART_B + PART_B, :] = total
     sent_z = [send(mid_s, got_z.at[d - 1], z_sem, d - 1, at(dz=d)) for d in range(1, NZ)]
 
     for copy in sent_c:
@@ -261,7 +278,7 @@
     total = mid_s[...]
     for d in range(1, NZ):
         total = total + got_z[d - 1]
-    out[c, y, x, PIECE : PIECE + PART_B, :] = total
+    out[c, y, x, PIECE : PIECE + 2 * PART_B, :] = total
     for copy in sent_d:
         copy.wait_recv()
 
@@ -271,37 +288,44 @@
     def second(d):
         return at(dx=d * c, dy=d * (1 - c))
 
-    def spread(block, n, along_first):
-        copies = []
-        if along_first:
-            copies += [send(block, block, e_sem, d - 1, first(d)) for d in range(1, 4)]
-        if n < 4:
-            copies += [send(block, block, f_sem, 3 * n + d - 1, second(d)) for d in range(1, 4)]
-        copies.append(send(block, block, g_sem, n, at(dc=1)))
-        return copies
-
-    own_block = out.at[c, y, x]
-    sent = spread(own_block, 0, True)
-    sent_e, sent_f, sent_g = sent[:3], sent[3:6], sent[6:]
-    for d in range(1, 4):
-        sent_e[d - 1].wait_recv()
-        block = out.at[c, (y + (4 - d) * c) % NY, (x + (4 - d) * (1 - c)) % NX]
-        more = spread(block, d, False)
-        sent_f += more[:3]
-        sent_g += more[3:]
-    for n in range(4):
-        for d in range(1, 4):
-            sent_f[3 * n + d - 1].wait_recv()
-            by = (y + (4 - n) * c + (4 - d) * (1 - c)) % NY
-            bx = (x + (4 - n) * (1 - c) + (4 - d) * c) % NX
-            sent_g += spread(out.at[c, by, bx], 4 + 3 * n + d - 1, False)
+    def gathered(n, d):
+        return out.at[c, (y + (4 - n) * c + (4 - d) * (1 - c)) % NY, (x + (4 - n) * (1 - c) + (4 - d) * c) % NX]
+
+    def swap(n, d):
+        block = gathered(n, d)
+        return send(block, block, g_sem, 4 * n + d, at(dc=1))
+
+    def both_ways(n):
+        block = gathered(n, 0)
+        return [send(block, block, f_sem, 3 * n + d - 1, second(d)) for d in (1, 3)]
+
+    own_block = gathered(0, 0)
+    sent_e = [send(own_block, own_block, e_sem, d - 1, first(d)) for d in range(1, 4)]
+    sent_f = {0: both_ways(0)}
+    sent_g = [swap(0, 0)]
+    for n in (1, 3, 2):
+        sent_e[n - 1].wait_recv()
+        sent_f[n] = both_ways(n)
+        sent_g.append(swap(n, 0))
+    passed = []
+    for n in (0, 1, 3, 2):
+        for d in (1, 3):
+            sent_f[n][d // 2].wait_recv()
+            block = gathered(n, d)
+            if d == (1, 3)[n % 2]:
+                passed.append((n, send(block, block, f_sem, 3 * n + 1, second(d))))
+            sent_g.append(swap(n, d))
+    for n, copy in passed:
+        copy.wait_recv()
+        sent_g.append(swap(n, 2))
+    sent_f = [copy for n in range(4) for copy in sent_f[n]] + [copy for _, copy in passed]
     for copy in sent_g:
         copy.wait_recv()
     for copy in sent_a + sent_b + sent_s + sent_c + sent_z + sent_d + sent_e + sent_f + sent_g:
         copy.wait_send()
 
 
-def sums(slab, omega, y_prev, prev_bs, slab_bs):
+def sums(slab, omega, y_prev, *marks):
     rows, cols = slab.shape
     chunks = cols // CHUNK
     vmem = pl.BlockSpec(memory_space=pltpu.VMEM)
@@ -311,25 +335,25 @@
     return pl.pallas_call(
         sums_kernel,
         out_shape=jax.ShapeDtypeStruct((NC, NY, NX, BLOCK, 128), f32),
-        in_specs=[hbm, hbm, vmem, vmem, vmem],
+        in_specs=[hbm, hbm] + [vmem] * 5,
         out_specs=vmem,
         scratch_shapes=[
             pltpu.VMEM((chunks, rows, CHUNK), f32),
             pltpu.VMEM((chunks, CHUNK, K), f32),
             pltpu.VMEM((SUMS, K), f32),
             pltpu.VMEM((rows, K), f32),
-            pltpu.VMEM((7, PART_A, 128), f32),
+            pltpu.VMEM((2, 7, PART_A, 128), f32),
             pltpu.VMEM((7, PIECE, 128), f32),
-            pltpu.VMEM((3, PART_B, 128), f32),
+            pltpu.VMEM((2, 3, PART_B, 128), f32),
             pltpu.VMEM((7, 8, 128), f32),
-            pltpu.VMEM((7, PART_B, 128), f32),
+            pltpu.VMEM((7, 2 * PART_B, 128), f32),
             pltpu.VMEM((PIECE, 128), f32),
-            pltpu.VMEM((PART_A, 128), f32),
-            pltpu.VMEM((PART_B, 128), f32),
+            pltpu.VMEM((2, PART_A, 128), f32),
+            pltpu.VMEM((2 * PART_B, 128), f32),
             dma((2, chunks)),
+            dma((2, 14)),
             dma((2, 7)),
-            dma((2, 7)),
-            dma((2, 3)),
+            dma((2, 6)),
             dma((2, 7)),
             dma((2, 7)),
             dma((2, 7)),
@@ -337,21 +361,24 @@
             dma((2, 12)),
             dma((2, 16)),
         ],
-        compiler_params=pltpu.CompilerParams(collective_id=0, has_side_effects=True, vmem_limit_bytes=63_500_000),
+        compiler_params=pltpu.CompilerParams(collective_id=0, has_side_effects=True, vmem_limit_bytes=62_900_000),
         cost_estimate=pl.CostEstimate(flops=60_000_000_000, bytes_accessed=10_000_000, transcendentals=0),
         name="sums",
-    )(slab, omega, y_prev, prev_bs, slab_bs)
-
-
-def factors_kernel(place, gathered, y_prev, q_prev, q_new, combined, xg, xs, u, us, ys, zs, ts, mapping):
+    )(slab, omega, y_prev, *(mark.reshape(2, 128) for mark in marks))
+
+
+def factors_kernel(gathered, y_prev, q_prev, q_new, combined, xg, xs, u, us, ys, zs, ts, mapping):
     for c in range(NC):
         lanes = slice(128 * c, 128 * c + 128)
         for y in range(NY):
             for x in range(NX):
                 ys[pl.ds(256 * y + PIECE * x, PIECE), lanes] = gathered[c, y, x, :PIECE, :]
-                zs[pl.ds(PART_A * y + PART_B * x, PART_B), lanes] = gathered[c, y, x, PIECE : PIECE + PART_B, :]
+                for half in (0, 1):
+                    start = half * (SUMS // 2) + (PART_A * x + PART_B * y if half else PART_A * y + PART_B * x)
+                    rows = gathered[c, y, x, PIECE + half * PART_B : PIECE + half * PART_B + PART_B, :]
+                    zs[pl.ds(start, PART_B), lanes] = rows
     for y in range(NY):
-        bs = gathered[0, y, 0, PIECE + PART_B :, :]
+        bs = gathered[0, y, 0, PIECE + 2 * PART_B :, :]
         for h in (0, 1):
             ts[:, 256 * y + 128 * h : 256 * y + 128 * h + 128] = table_of(bs[h : h + 1], bs[h + 2 : h + 3])
     new = ys[...]
@@ -367,7 +394,8 @@
     core = mm(mm(u[...], inner, ((1,), (1,))), inner)
     found = mm(core, zs[:L, :], ((1,), (1,)))
     mapping[...] = found
-    y_place = place[0]
+    y_place = lax.axis_index("y")
+    col = lax.axis_index(COL)
     cols = pl.ds(pl.multiple_of(y_place * 256, 256), 256)
     table = ts[:, cols]
     high = found.astype(jnp.bfloat16)
@@ -377,27 +405,28 @@
     combined[:, :256] = mul(high, table) + (mul(mid, table) + mul(low, table))
     combined[:, 256:] = mapping[:, pl.ds(pl.multiple_of(y_place * 128, 128), 128)]
     q_prev[...] = mm(y_prev[...], outer, ((1,), (1,)))
-    q_new[...] = mm(ys[pl.ds(pl.multiple_of(place[1] * 8, 8), 8), :], outer, ((1,), (1,)))
-
-
-def factors(place, gathered, y_prev):
+    pair = mm(ys[pl.ds(pl.multiple_of(y_place * 256 + (col // 2) * 8, 8), 8), :], outer, ((1,), (1,)))
+    q_new[...] = jnp.where(col % 2 == 0, pair[:4], pair[4:])
+
+
+def factors(gathered, y_prev):
     vmem = pl.BlockSpec(memory_space=pltpu.VMEM)
     f32 = jnp.float32
     return pl.pallas_call(
         factors_kernel,
         out_shape=(
             jax.ShapeDtypeStruct(y_prev.shape, f32),
-            jax.ShapeDtypeStruct((8, K), f32),
+            jax.ShapeDtypeStruct((4, K), f32),
             jax.ShapeDtypeStruct((K, 384), f32),
         ),
-        in_specs=[pl.BlockSpec(memory_space=pltpu.SMEM), vmem, vmem],
+        in_specs=[vmem, vmem],
         out_specs=[vmem] * 3,
         scratch_shapes=[pltpu.VMEM((K, K), f32)] * 4
         + [pltpu.VMEM((1024, K), f32), pltpu.VMEM((SUMS, K), f32), pltpu.VMEM((L, 1024), jnp.bfloat16), pltpu.VMEM((K, L), f32)],
         compiler_params=pltpu.CompilerParams(vmem_limit_bytes=40 * 2**20),
         cost_estimate=pl.CostEstimate(flops=20_000_000_000, bytes_accessed=3_000_000, transcendentals=0),
         name="factors",
-    )(place, gathered, y_prev)
+    )(gathered, y_prev)
 
 
 def core_kernel(combined, slab, w_prev, out, terms, far_l, far_r, near_l, near_r, far_sem, near_sem):
@@ -484,20 +513,10 @@
     )(combined, slab, w_prev)
 
 
-def as_rows(bucket, sign):
-    rows = jnp.concatenate([bucket.reshape(2, 128), sign.reshape(2, 128)]).astype(jnp.float32)
-    return jnp.concatenate([rows, jnp.zeros((4, 128), jnp.float32)])
-
-
 def on_device(slab, omega, y_prev, w_prev, prev_bucket, prev_sign, slab_bucket, slab_sign):
-    y = lax.axis_index("y")
-    col = lax.axis_index(COL)
-    gathered = sums(slab, omega, y_prev, as_rows(prev_bucket, prev_sign), as_rows(slab_bucket, slab_sign))
-    place = jnp.stack([y, y * 32 + col // 2]).astype(jnp.int32)
-    q_prev, q_pair, combined = factors(place, gathered, y_prev)
-    q_new = lax.dynamic_slice_in_dim(q_pair, (col % 2) * 4, 4, 0)
-    x_core = core_product(combined, slab, w_prev)
-    return (q_prev, q_new, x_core)
+    gathered = sums(slab, omega, y_prev, prev_bucket, prev_sign, slab_bucket, slab_sign)
+    q_prev, q_new, combined = factors(gathered, y_prev)
+    return (q_prev, q_new, core_product(combined, slab, w_prev))
 
 
 def solution(mesh):

time: 109 us -> 104 us (0.954)
  Pallas kernels: 103 us -> 101 us
  local copies, waits for them, and re-layouts: 4.31 us -> 2.52 us
  other arithmetic: 1.49 us -> 0 us
    pallas_call x1, Pallas kernels: 48.7 us -> 46.8 us  [sums(): pl.pallas_call(sums_kernel, out_shape=jax.ShapeDtypeStruct((NC, NY, NX, B...]
    convert_element_type x2 -> x0, other arithmetic: 1.42 us -> none  [as_rows(): jnp.concatenate([bucket.reshape(2, 128), sign.reshape(2, 128)])]
    concatenate x2 -> x0, local copies, waits for them, and re-layouts: 1.2 us -> none  [as_rows(): return jnp.concatenate([rows, jnp.zeros((4, 128), jnp.float32)])]
where the time goes in v3:
time: 104 us
  Pallas kernels  101 us (97%)
  local copies, waits for them, and re-layouts  2.52 us (2%)
    pallas_call x1, Pallas kernels, sums(): pl.pallas_call(sums_kernel, out_shape=jax.ShapeDtypeStruct((NC, NY, NX, B...  46.8 us
    pallas_call x1, Pallas kernels, core_product(): pl.pallas_call(core_kernel, out_shape=jax.ShapeDtypeStruct((rows, cols),...  37.6 us
    pallas_call x1, Pallas kernels, factors(): pl.pallas_call(factors_kernel, out_shape=(jax.ShapeDtypeStruct(y_prev.sha...  16.1 us
    unnamed x9, local copies, waits for them, and re-layouts  2.52 us

profile of v3, /device:TPU:1, one launch (start us, length us, event | category | flops | bytes accessed | tf_op | source)
XLA Modules:
  0.0 103.8 jit_solution(9784801658785359769)
XLA Ops:
  0.6 0.0 copy-start.2
  0.6 46.8 %sums.1.gathered = f32[2,4,4,120,128]{4,3,2,1,0:T(8,128)} custom-call(f32[256,4096]{1,0:T(8,128)} %slab.3, f32[4096,256]{1,0:T(8,128)} %omega.1, f32[256,256]{1,0:T(8,128)} %y_prev.3, s32[2,128]{1,0:T(2,128)} %bitcast.4, s32[2,128]{1,0:T(2,128)} %bitcast.5, s32[2,128]{1,0:T(2,128)} %bitcast.6, s32[2,128]{1,0:T(2,128)} %bitcast.7), custom_call_target="tpu_custom_call" | custom-call | flops 60000002048 | bytes 10000000 | tf_op jit(solution)/shard_map/sums/pallas_call | solution.py:335
  47.5 0.0 copy-done.2
  47.5 0.0 copy-start.3
  47.5 1.5 %copy-done.3 = f32[2,4,4,120,128]{4,3,2,1,0:T(8,128)S(1)} copy-done((f32[2,4,4,120,128]{4,3,2,1,0:T(8,128)S(1)}, f32[2,4,4,120,128]{4,3,2,1,0:T(8,128)}, u32[]{:S(2)}) %copy-start.3) | copy-done | bytes 1966104
  49.0 0.0 copy-start
  49.0 0.0 copy-start.1
  49.0 16.1 %factors.1 = (f32[256,256]{1,0:T(8,128)}, f32[4,256]{1,0:T(4,128)}, f32[256,384]{1,0:T(8,128)S(1)}) custom-call(f32[2,4,4,120,128]{4,3,2,1,0:T(8,128)S(1)} %copy-done.3, f32[256,256]{1,0:T(8,128)S(1)} %copy-done.2), custom_call_target="tpu_custom_call" | custom-call | flops 20000000000 | bytes 3000000 | tf_op jit(solution)/shard_map/factors/pallas_call | solution.py:415
  65.1 0.0 copy-done
  65.2 0.0 copy-done.1
  65.2 37.6 %core_product.1 = f32[64,4096]{1,0:T(8,128)S(1)} custom-call(f32[256,384]{1,0:T(8,128)S(1)} %get-tuple-element.8.combined, f32[256,4096]{1,0:T(8,128)S(1)} %copy-done, f32[128,4096]{1,0:T(8,128)S(1)} %copy-done.1), custom_call_target="tpu_custom_call" | custom-call | flops 60000002048 | bytes 10000000 | tf_op jit(solution)/shard_map/core_product/pallas_call | solution.py:496
  102.8 1.0 copy.12
Async XLA Ops:
  0.6 46.8 %copy-start.2 = (f32[256,256]{1,0:T(8,128)S(1)}, f32[256,256]{1,0:T(8,128)}, u32[]{:S(2)}) copy-start(f32[256,256]{1,0:T(8,128)} %y_prev.3) | copy-start | bytes 786436
  47.5 1.5 %copy-start.3 = (f32[2,4,4,120,128]{4,3,2,1,0:T(8,128)S(1)}, f32[2,4,4,120,128]{4,3,2,1,0:T(8,128)}, u32[]{:S(2)}) copy-start(f32[2,4,4,120,128]{4,3,2,1,0:T(8,128)} %sums.1.gathered) | copy-start | bytes 5898244
  49.0 16.1 %copy-start = (f32[256,4096]{1,0:T(8,128)S(1)}, f32[256,4096]{1,0:T(8,128)}, u32[]{:S(2)}) copy-start(f32[256,4096]{1,0:T(8,128)} %slab.3) | copy-start | bytes 12582916
  49.0 16.1 %copy-start.1 = (f32[128,4096]{1,0:T(8,128)S(1)}, f32[128,4096]{1,0:T(8,128)}, u32[]{:S(2)}) copy-start(f32[128,4096]{1,0:T(8,128)} %w_prev.1) | copy-start | bytes 6291460

commit v4 on v3

v4 whole, which is shorter than its diff:
```python
import jax
import jax.numpy as jnp
from jax import lax
from jax.experimental import pallas as pl
from jax.experimental.pallas import tpu as pltpu
from jax.sharding import Mesh
from jax.sharding import PartitionSpec as P

L = 512
COL = ("z", "x", "core")
ROW_COL = ("y", "z", "x", "core")
MESH = pl.DeviceIdType.MESH
highest = lax.Precision.HIGHEST
K = 256
BLK = 16
SUP = 64


def mm(a, b, dims=((1,), (0,))):
    return lax.dot_general(a, b, (dims, ((), ())), precision=highest, preferred_element_type=jnp.float32)


def eliminate(panel, k):
    off = k * BLK
    tile = off // 128 * 128
    cols = []
    for j in range(BLK):
        c = off + j
        cols.append([jnp.broadcast_to(panel[h * 8 : h * 8 + 8, c : c + 1], (8, 128)) for h in (0, 1)])
    lane = lax.broadcasted_iota(jnp.int32, (8, K), 1)
    row = lax.broadcasted_iota(jnp.int32, (8, K), 0)
    row1 = lax.broadcasted_iota(jnp.int32, (8, 128), 0)
    inside = (lane >= off) & (lane < off + BLK)
    top = jnp.where(inside, (lane == row + off).astype(jnp.float32), panel[:8])
    bot = jnp.where(inside, (lane == row + off + 8).astype(jnp.float32), panel[8:])
    lane1 = lax.broadcasted_iota(jnp.int32, (8, 128), 1) + tile
    corner = [jnp.zeros((8, 128), jnp.float32), jnp.zeros((8, 128), jnp.float32)]
    scales = []
    for j in range(BLK):
        h, r = divmod(j, 8)
        mine = cols[j]
        pivot = jnp.broadcast_to(mine[h][r : r + 1], (8, 128))
        rs = lax.rsqrt(pivot)
        inv = rs * rs
        scales.append(rs)
        low = mine[1] * inv
        high = None
        if h == 0:
            high = mine[0] * inv
        for m in range(j + 1, BLK):
            hm, rm = divmod(m, 8)
            u = jnp.broadcast_to(mine[hm][rm : rm + 1], (8, 128))
            cols[m][1] = cols[m][1] - low * u
            if hm == 0:
                cols[m][0] = cols[m][0] - high * u
        if h == 0:
            p = jnp.broadcast_to(top[r : r + 1], (8, K))
            hm_ = jnp.where(row1 > r, high, 0.0)
            top = top - jnp.concatenate([hm_, hm_], axis=1) * p
            bot = bot - jnp.concatenate([low, low], axis=1) * p
        else:
            p = jnp.broadcast_to(bot[r : r + 1], (8, K))
            lm_ = jnp.where(row1 > r, low, 0.0)
            bot = bot - jnp.concatenate([lm_, lm_], axis=1) * p
    st = jnp.zeros((8, 128), jnp.float32)
    sb = jnp.zeros((8, 128), jnp.float32)
    for j in range(8):
        st = jnp.where(row1 == j, scales[j], st)
        sb = jnp.where(row1 == j, scales[j + 8], sb)
    top = top * jnp.concatenate([st, st], axis=1)
    bot = bot * jnp.concatenate([sb, sb], axis=1)
    for j in range(BLK):
        for h in (0, 1):
            keep = (lane1 == off + j) & (row1 + 8 * h >= j)
            corner[h] = jnp.where(keep, cols[j][h] * scales[j], corner[h])
    return jnp.concatenate([top, bot], axis=0), jnp.concatenate(corner, axis=0)


def factor_step(w, u, k):
    off = k * BLK
    rows = slice(off, off + BLK)
    panel, corner = eliminate(w[rows, :], k)
    tile = off // 128 * 128
    w[rows, :] = panel
    lane = lax.broadcasted_iota(jnp.int32, (BLK, K), 1)
    upper = jnp.where(lane >= off + BLK, panel, 0.0)
    u[rows, :] = upper
    sup_end = (off // SUP + 1) * SUP
    if off + BLK < sup_end:
        turned = panel[:, tile : tile + 128].T
        left = turned[off + BLK - tile : sup_end - tile]
        rest = slice(off + BLK, sup_end)
        lane2 = lax.broadcasted_iota(jnp.int32, (sup_end - off - BLK, K), 1)
        old = jnp.where((lane2 >= off) & (lane2 < off + BLK), 0.0, w[rest, :])
        w[rest, :] = old - mm(left, panel)
    elif sup_end < K:
        start = sup_end - SUP
        block = w[start:sup_end, :]
        t0 = sup_end // 128 * 128
        turned = block[:, t0:].T
        left = turned[sup_end - t0 :]
        rest = slice(sup_end, K)
        lane2 = lax.broadcasted_iota(jnp.int32, (K - sup_end, K), 1)
        old = jnp.where((lane2 >= start) & (lane2 < sup_end), 0.0, w[rest, :])
        lane3 = lax.broadcasted_iota(jnp.int32, (SUP, K), 1)
        row3 = lax.broadcasted_iota(jnp.int32, (SUP, K), 0) + start
        block = jnp.where((lane3 < sup_end) & (lane3 > row3), 0.0, block)
        w[rest, :] = old - mm(left, block)
    return corner


def factor_both(wg, ws, ug, us, after):
    for k in range(K // BLK):
        cg = factor_step(wg, ug, k)
        factor_step(ws, us, k)
        off = k * BLK
        tile = off // 128 * 128
        rows = slice(off, off + BLK)
        turned = cg.T[off - tile : off - tile + BLK]
        ug[rows, off:off + BLK] = turned
        after(k)


NZ, NX, NC, NY = 8, 4, 2, 4
CHUNK = 512
SUMS = L + K
PART_A = SUMS // 2 // NY
PART_B = PART_A // NX
PIECE = K // NX
BLOCK = PIECE + 2 * PART_B + 8


def split(v):
    high = v.astype(jnp.bfloat16)
    return high, (v - high.astype(jnp.float32)).astype(jnp.bfloat16)


def mul(a, b, dims=((1,), (0,))):
    return lax.dot_general(a, b, (dims, ((), ())), preferred_element_type=jnp.float32)


def mul3(a, b, dims=((1,), (0,))):
    ah, al = split(a)
    bh, bl = split(b)
    return mul(ah, bh, dims) + (mul(ah, bl, dims) + mul(al, bh, dims))


def signed_sum(table, v):
    high = v.astype(jnp.bfloat16)
    rest = v - high.astype(jnp.float32)
    mid = rest.astype(jnp.bfloat16)
    low = (rest - mid.astype(jnp.float32)).astype(jnp.bfloat16)
    return mul(table, high) + (mul(table, mid) + mul(table, low))


def table_of(bucket, sign):
    level = lax.broadcasted_iota(jnp.int32, (L, bucket.shape[1]), 0).astype(jnp.float32)
    return jnp.where(level == bucket, 2.0 * sign - 1.0, 0.0).astype(jnp.bfloat16)


def whole_kernel(slab, omega, y_prev, w_prev, prev_bucket, prev_sign, slab_bucket, slab_sign, q_prev, q_new, x_core,
                 out, slab_v, omega_v, w_v, stack, part, got_sums, got_part, chip_sums, chip_part, got_a, got_b, got_s,
                 got_c, got_z, mid_p, mid_a, mid_s, xg, xs, u, us, ys, zs, ts, comb, comb_v, core, mapping,
                 early, v_far, v_up, v_down, terms, far_l, far_r, near_l, near_r, found_v, pass_up, pass_down,
                 load_sem, swap_sem, a_sem, b_sem, s_sem, c_sem, z_sem, d_sem, e_sem, f_sem, g_sem, v_sem, x_sem, far_sem, near_sem):
    z, x, c, y = (lax.axis_index(name) for name in ("z", "x", "core", "y"))

    def at(dz=0, dx=0, dc=0, dy=0):
        return {"z": (z + dz) % NZ, "x": (x + dx) % NX, "core": (c + dc) % NC, "y": (y + dy) % NY}

    def send(src, dst, sems, i, where):
        copy = pltpu.make_async_remote_copy(
            src_ref=src, dst_ref=dst, send_sem=sems.at[0, i], recv_sem=sems.at[1, i], device_id=where, device_id_type=MESH
        )
        copy.start()
        return copy

    barrier = pltpu.get_barrier_semaphore()
    peers = [at(dz=d) for d in range(1, NZ)]
    peers += [at(dy=d) for d in range(1, NY)] + [at(dx=d) for d in range(1, NX)] + [at(dc=1)]
    for peer in peers:
        pl.semaphore_signal(barrier, inc=1, device_id=peer, device_id_type=MESH)

    chunks = slab_v.shape[0]
    loads = []
    for i in range(chunks):
        loads.append(pltpu.make_async_copy(slab.at[:, pl.ds(i * CHUNK, CHUNK)], slab_v.at[i], load_sem.at[0, i]))
        loads.append(pltpu.make_async_copy(omega.at[pl.ds(i * CHUNK, CHUNK), :], omega_v.at[i], load_sem.at[1, i]))
    for load in loads:
        load.start()
    for i in range(chunks):
        pltpu.make_async_copy(w_prev.at[:, pl.ds(i * CHUNK, CHUNK)], w_v.at[i], load_sem.at[2, i]).start()

    def real(ref):
        return ref[...].astype(jnp.float32)

    bucket, sign = real(prev_bucket), real(prev_sign)
    table = jnp.concatenate([table_of(bucket[h : h + 1], sign[h : h + 1]) for h in (0, 1)], axis=1)
    own = y_prev[...]
    stack[:L, :] = signed_sum(table, own)
    stack[L:, :] = mm(own, own, ((0,), (0,)))
    out[c, y, x, PIECE + 2 * PART_B :, :] = jnp.concatenate([real(slab_bucket), real(slab_sign), jnp.zeros((4, 128), jnp.float32)])
    part[...] = jnp.zeros_like(part)

    def multiply(i):
        pltpu.make_async_copy(slab.at[:, pl.ds(0, CHUNK)], slab_v.at[i], load_sem.at[0, i]).wait()
        pltpu.make_async_copy(omega.at[pl.ds(0, CHUNK), :], omega_v.at[i], load_sem.at[1, i]).wait()
        part[...] += mul3(slab_v[i], omega_v[i])

    pl.loop(0, chunks)(multiply)
    pl.semaphore_wait(barrier, len(peers))

    ours = pl.ds(pl.multiple_of(c * 128, 128), 128)
    theirs = pl.ds(pl.multiple_of((1 - c) * 128, 128), 128)
    swap_sums = send(stack.at[:, theirs], got_sums, swap_sem, 0, at(dc=1))
    swap_part = send(part.at[:, theirs], got_part, swap_sem, 1, at(dc=1))

    def share(half, where):
        place = where["x"] if half else where["y"]
        return pl.ds(pl.multiple_of(half * (SUMS // 2) + place * PART_A, 8), PART_A)

    swap_sums.wait_recv()
    chip_sums[...] = stack[:, ours] + got_sums[...]
    sent_a = []
    for d in (2, 1, 3):
        for half in (0, 1):
            where = at(dx=d) if half else at(dy=d)
            sent_a.append(send(chip_sums.at[share(half, where), :], got_a.at[half, d - 1], a_sem, 2 * (d - 1) + half, where))

    swap_part.wait_recv()
    chip_part[...] = part[:, ours] + got_part[...]
    sent_b = []
    for d in (2, 1, 3):
        where = at(dx=d)
        piece = chip_part.at[pl.ds(pl.multiple_of(where["x"] * PIECE, 8), PIECE), :]
        sent_b.append(send(piece, got_b.at[d - 1], b_sem, d - 1, where))

    for copy in sent_a:
        copy.wait_recv()
    for half in (0, 1):
        total = chip_sums[share(half, at()), :]
        for d in range(1, 4):
            total = total + got_a[half, d - 1]
        mid_a[half] = total
    sent_s = []
    for d in range(1, NX):
        for half in (0, 1):
            where = at(dy=d) if half else at(dx=d)
            place = where["y"] if half else where["x"]
            piece = mid_a.at[half, pl.ds(pl.multiple_of(place * PART_B, 8), PART_B), :]
            sent_s.append(send(piece, got_s.at[half, d - 1], s_sem, 2 * (d - 1) + half, where))

    for copy in sent_b:
        copy.wait_recv()
    total = chip_part[pl.ds(pl.multiple_of(x * PIECE, 8), PIECE), :]
    for d in range(1, NX):
        total = total + got_b[d - 1]
    mid_p[...] = total
    sent_c = []
    for d in range(1, NZ):
        where = at(dz=d)
        piece = mid_p.at[pl.ds(pl.multiple_of(where["z"] * 8, 8), 8), :]
        sent_c.append(send(piece, got_c.at[d - 1], c_sem, d - 1, where))

    for copy in sent_s:
        copy.wait_recv()
    for half in (0, 1):
        total = mid_a[half, pl.ds(pl.multiple_of((y if half else x) * PART_B, 8), PART_B), :]
        for d in range(1, NX):
            total = total + got_s[half, d - 1]
        mid_s[half * PART_B : half * PART_B + PART_B, :] = total
    sent_z = [send(mid_s, got_z.at[d - 1], z_sem, d - 1, at(dz=d)) for d in range(1, NZ)]

    for copy in sent_c:
        copy.wait_recv()
    total = mid_p[pl.ds(pl.multiple_of(z * 8, 8), 8), :]
    for d in range(1, NZ):
        total = total + got_c[d - 1]
    tile = pl.ds(pl.multiple_of(z * 8, 8), 8)
    out[c, y, x, tile, :] = total
    sent_d = [send(out.at[c, y, x, tile, :], out.at[c, y, x, tile, :], d_sem, d - 1, at(dz=d)) for d in range(1, NZ)]

    for copy in sent_z:
        copy.wait_recv()
    total = mid_s[...]
    for d in range(1, NZ):
        total = total + got_z[d - 1]
    out[c, y, x, PIECE : PIECE + 2 * PART_B, :] = total
    for copy in sent_d:
        copy.wait_recv()

    def first(d):
        return at(dx=d * (1 - c), dy=d * c)

    def second(d):
        return at(dx=d * c, dy=d * (1 - c))

    def gathered(n, d):
        return out.at[c, (y + (4 - n) * c + (4 - d) * (1 - c)) % NY, (x + (4 - n) * (1 - c) + (4 - d) * c) % NX]

    def swap(n, d):
        block = gathered(n, d)
        return send(block, block, g_sem, 4 * n + d, at(dc=1))

    def both_ways(n):
        block = gathered(n, 0)
        return [send(block, block, f_sem, 3 * n + d - 1, second(d)) for d in (1, 3)]

    own_block = gathered(0, 0)
    sent_e = [send(own_block, own_block, e_sem, d - 1, first(d)) for d in range(1, 4)]
    sent_f = {0: both_ways(0)}
    sent_g = [swap(0, 0)]
    for n in (1, 3, 2):
        sent_e[n - 1].wait_recv()
        sent_f[n] = both_ways(n)
        sent_g.append(swap(n, 0))
    passed = []
    for n in (0, 1, 3, 2):
        for d in (1, 3):
            sent_f[n][d // 2].wait_recv()
            block = gathered(n, d)
            if d == (1, 3)[n % 2]:
                passed.append((n, send(block, block, f_sem, 3 * n + 1, second(d))))
            sent_g.append(swap(n, d))
    for n, copy in passed:
        copy.wait_recv()
        sent_g.append(swap(n, 2))
    sent_f = [copy for n in range(4) for copy in sent_f[n]] + [copy for _, copy in passed]
    for copy in sent_g:
        copy.wait_recv()
    everything = [swap_sums, swap_part] + sent_a + sent_b + sent_s + sent_c + sent_z + sent_d + sent_e + sent_f + sent_g

    for cc in range(NC):
        lanes = slice(128 * cc, 128 * cc + 128)
        for yy in range(NY):
            for xx in range(NX):
                ys[pl.ds(256 * yy + PIECE * xx, PIECE), lanes] = out[cc, yy, xx, :PIECE, :]
                for half in (0, 1):
                    start = half * (SUMS // 2) + (PART_A * xx + PART_B * yy if half else PART_A * yy + PART_B * xx)
                    zs[pl.ds(start, PART_B), lanes] = out[cc, yy, xx, PIECE + half * PART_B : PIECE + half * PART_B + PART_B, :]
    for yy in range(NY):
        marks = out[0, yy, 0, PIECE + 2 * PART_B :, :]
        for h in (0, 1):
            ts[yy, :, 128 * h : 128 * h + 128] = table_of(marks[h : h + 1], marks[h + 2 : h + 3])
    new = ys[...]
    xg[...] = zs[L:, :] + mm(new, new, ((0,), (0,)))
    sketch = zs[:L, :]
    for yy in range(NY):
        sketch = sketch + signed_sum(ts[yy], ys[256 * yy : 256 * yy + 256, :])
    zs[:L, :] = sketch

    up, across, down = (y + 1) % NY, (y + 2) % NY, (y + 3) % NY
    mine = pl.ds(pl.multiple_of(y * 128, 128), 128)
    for i in range(chunks):
        pltpu.make_async_copy(w_prev.at[:, pl.ds(0, CHUNK)], w_v.at[i], load_sem.at[2, i]).wait()
    high = sketch.astype(jnp.bfloat16)
    rest = sketch - high.astype(jnp.float32)
    mid = rest.astype(jnp.bfloat16)
    low = (rest - mid.astype(jnp.float32)).astype(jnp.bfloat16)
    table = ts[y]
    over = ((0,), (0,))
    comb_v[:, :256] = mul(high, table, over) + (mul(mid, table, over) + mul(low, table, over))
    comb_v[:, 256:] = zs[mine, :].T

    def data(n):
        return jnp.concatenate([slab_v[n], w_v[n]], axis=0)

    def along(src, dst, sems, i, peer):
        return send(src, dst, sems, i, at(dy=peer))

    front, back = slice(0, K // 2), slice(K // 2, K)
    early[2] = mul3(comb_v[...], data(across))
    moves = [
        along(early.at[2, front, :], v_far.at[0], v_sem, 0, 1),
        along(early.at[2, back, :], v_far.at[1], v_sem, 1, 3),
    ]
    early[1] = mul3(comb_v[...], data(up))
    moves.append(along(early.at[1, back, :], v_up.at[back, :], v_sem, 2, 1))
    early[3] = mul3(comb_v[...], data(down))
    moves.append(along(early.at[3, front, :], v_down.at[front, :], v_sem, 3, 3))
    early[0] = mul3(comb_v[...], data(y))

    def after(k):
        if k != 10:
            return
        moves[0].wait_recv()
        early[1, front, :] = early[1, front, :] + v_far[0]
        moves.append(along(early.at[1, front, :], v_up.at[front, :], v_sem, 4, 1))
        moves[1].wait_recv()
        early[3, back, :] = early[3, back, :] + v_far[1]
        moves.append(along(early.at[3, back, :], v_down.at[back, :], v_sem, 5, 3))

    xs[...] = mm(sketch, sketch, over)
    factor_both(xg, xs, u, us, after)
    row = lax.broadcasted_iota(jnp.int32, (K, K), 0)
    lane = lax.broadcasted_iota(jnp.int32, (K, K), 1)
    inner = jnp.where(lane <= row, xs[...], 0.0)
    core[...] = mm(mm(u[...], inner, ((1,), (1,))), inner)
    found = mm(core[...], zs[:L, :], ((1,), (1,)))
    mapping[...] = found
    high = found.astype(jnp.bfloat16)
    rest = found - high.astype(jnp.float32)
    mid = rest.astype(jnp.bfloat16)
    low = (rest - mid.astype(jnp.float32)).astype(jnp.bfloat16)
    table = ts[y]
    comb[:, :256] = mul(high, table) + (mul(mid, table) + mul(low, table))
    comb[:, 256:] = mapping[:, mine]

    rows = x_core.shape[0]
    late = chunks - NY
    half = late // 2

    def spot(place):
        return pl.ds(pl.multiple_of(place * rows, 8), rows)

    far = {}
    for n in [n for i in range(half) for n in (i, half + i)]:
        terms[n] = mul3(comb[...], data(NY + n))
        left = n < half
        far[n] = along(terms.at[n, spot(across), :], far_l.at[n] if left else far_r.at[n - half], far_sem, n, 1 if left else 3)
    to_up, to_down = {}, {}

    def near(n, upward):
        if upward:
            to_up[n] = along(terms.at[n, spot(up), :], near_l.at[n], near_sem, n, 1)
        else:
            to_down[n] = along(terms.at[n, spot(down), :], near_r.at[n], near_sem, late + n, 3)

    for i in range(half):
        near(half + i, True)
        near(i, False)

    for copy in moves[2:]:
        copy.wait_recv()
    found_v[...] = mm(core[...], early[0] + (v_up[...] + v_down[...]))

    def columns(place, start, size):
        return pl.ds(pl.multiple_of(place * CHUNK + start, 128), size)

    wide = CHUNK // 2
    relay_up = along(found_v.at[spot(across), 0:wide], pass_up, x_sem, 0, 1)
    relay_down = along(found_v.at[spot(across), wide:CHUNK], pass_down, x_sem, 1, 3)
    home = [
        along(found_v.at[spot(up), :], x_core.at[:, columns(y, 0, CHUNK)], x_sem, 2, 1),
        along(found_v.at[spot(down), :], x_core.at[:, columns(y, 0, CHUNK)], x_sem, 3, 3),
    ]
    for i in range(half):
        far[i].wait_recv()
        terms[i, spot(up), :] = terms[i, spot(up), :] + far_l[i]
        near(i, True)
        far[half + i].wait_recv()
        terms[half + i, spot(down), :] = terms[half + i, spot(down), :] + far_r[i]
        near(half + i, False)
    relay_up.wait_recv()
    home.append(along(pass_up, x_core.at[:, columns(down, 0, wide)], x_sem, 4, 1))
    relay_down.wait_recv()
    home.append(along(pass_down, x_core.at[:, columns(up, wide, wide)], x_sem, 5, 3))
    x_core[:, columns(y, 0, CHUNK)] = found_v[spot(y), :]

    outer = jnp.where(lane <= row, xg[...], 0.0)
    q_prev[...] = mm(y_prev[...], outer, ((1,), (1,)))
    col = (z * NX + x) * NC + c
    pair = mm(ys[pl.ds(pl.multiple_of(y * 256 + (col // 2) * 8, 8), 8), :], outer, ((1,), (1,)))
    q_new[...] = jnp.where(col % 2 == 0, pair[:4], pair[4:])

    for i in range(half):
        for n in (half + i, i):
            to_up[n].wait_recv()
            to_down[n].wait_recv()
            x_core[:, (NY + n) * CHUNK : (NY + n + 1) * CHUNK] = terms[n, spot(y), :] + (near_l[n] + near_r[n])
    for copy in home:
        copy.wait_recv()
    everything += moves + [relay_up, relay_down] + home + list(far.values()) + list(to_up.values()) + list(to_down.values())
    for copy in everything:
        copy.wait_send()


def whole(slab, omega, y_prev, w_prev, *marks):
    rows, cols = slab.shape
    chunks = cols // CHUNK
    late = chunks - NY
    share = K // NY
    vmem = pl.BlockSpec(memory_space=pltpu.VMEM)
    hbm = pl.BlockSpec(memory_space=pltpu.HBM)
    f32 = jnp.float32
    dma = pltpu.SemaphoreType.DMA

    def buffers(*shapes):
        return [pltpu.VMEM(shape, f32) for shape in shapes]

    return pl.pallas_call(
        whole_kernel,
        out_shape=(
            jax.ShapeDtypeStruct(y_prev.shape, f32),
            jax.ShapeDtypeStruct((4, K), f32),
            jax.ShapeDtypeStruct((share, cols), f32),
        ),
        in_specs=[hbm, hbm, vmem, hbm] + [vmem] * 4,
        out_specs=[vmem] * 3,
        scratch_shapes=buffers(
            (NC, NY, NX, BLOCK, 128),
            (chunks, rows, CHUNK),
            (chunks, CHUNK, K),
            (chunks, w_prev.shape[0], CHUNK),
            (SUMS, K),
            (rows, K),
            (SUMS, 128),
            (rows, 128),
            (SUMS, 128),
            (rows, 128),
            (2, 3, PART_A, 128),
            (3, PIECE, 128),
            (2, 3, PART_B, 128),
            (7, 8, 128),
            (7, 2 * PART_B, 128),
            (PIECE, 128),
            (2, PART_A, 128),
            (2 * PART_B, 128),
            (K, K),
            (K, K),
            (K, K),
            (K, K),
            (1024, K),
            (SUMS, K),
        )
        + [pltpu.VMEM((NY, L, K), jnp.bfloat16)]
        + buffers(
            (K, 384),
            (K, 384),
            (K, K),
            (K, L),
            (NY, K, CHUNK),
            (2, K // 2, CHUNK),
            (K, CHUNK),
            (K, CHUNK),
            (late, K, CHUNK),
            (late // 2, share, CHUNK),
            (late // 2, share, CHUNK),
            (late, share, CHUNK),
            (late, share, CHUNK),
            (K, CHUNK),
            (share, CHUNK // 2),
            (share, CHUNK // 2),
        )
        + [
            dma((3, chunks)),
            dma((2, 2)),
            dma((2, 6)),
            dma((2, 3)),
            dma((2, 6)),
            dma((2, 7)),
            dma((2, 7)),
            dma((2, 7)),
            dma((2, 3)),
            dma((2, 12)),
            dma((2, 16)),
            dma((2, 6)),
            dma((2, 6)),
            dma((2, late)),
            dma((2, 2 * late)),
        ],
        compiler_params=pltpu.CompilerParams(collective_id=0, has_side_effects=True, vmem_limit_bytes=67_043_328),
        cost_estimate=pl.CostEstimate(flops=60_000_000_000, bytes_accessed=20_000_000, transcendentals=0),
        name="whole",
    )(slab, omega, y_prev, w_prev, *(mark.reshape(2, 128) for mark in marks))


def solution(mesh):
    finer = Mesh(mesh.devices.reshape(NZ, NX, NC, NY), ("z", "x", "core", "y"))
    return jax.shard_map(
        whole,
        mesh=finer,
        in_specs=(
            P("y", COL),
            P(COL, None),
            P(ROW_COL, None),
            P("y", COL),
            P(ROW_COL),
            P(ROW_COL),
            P("y"),
            P("y"),
        ),
        out_specs=(P(ROW_COL, None), P(ROW_COL, None), P("y", COL)),
        check_vma=False,
    )
```

time: 104 us -> 98.1 us (0.943)
  Pallas kernels: 101 us -> 92 us
  local copies, waits for them, and re-layouts: 2.52 us -> 5.21 us
    pallas_call x3 -> x1, Pallas kernels: 101 us -> 92 us  [whole(): pl.pallas_call(whole_kernel, out_shape=(jax.ShapeDtypeStruct(y_prev.shape...]
    unnamed x9 -> x3, local copies, waits for them, and re-layouts: 2.52 us -> 5.21 us
where the time goes in v4:
time: 98.1 us; the launch traced here: 97.9 us
  Pallas kernels  92 us (94%)
  local copies, waits for them, and re-layouts  5.21 us (5%)
    pallas_call x1, Pallas kernels, whole(): pl.pallas_call(whole_kernel, out_shape=(jax.ShapeDtypeStruct(y_prev.shape...  92 us
    unnamed x3, local copies, waits for them, and re-layouts  5.21 us

profile of v4, /device:TPU:1, one launch (start us, length us, event | category | flops | bytes accessed | tf_op | source)
XLA Modules:
  0.0 97.9 jit_solution(5553116171855027128)
XLA Ops:
  0.6 92.0 %whole.1 = (f32[256,256]{1,0:T(8,128)}, f32[4,256]{1,0:T(4,128)}, f32[64,4096]{1,0:T(8,128)}) custom-call(f32[256,4096]{1,0:T(8,128)} %slab.1, f32[4096,256]{1,0:T(8,128)} %omega.1, f32[256,256]{1,0:T(8,128)} %y_prev.1, f32[128,4096]{1,0:T(8,128)} %w_prev.1, s32[2,128]{1,0:T(2,128)} %bitcast.4, s32[2,128]{1,0:T(2,128)} %bitcast.5, s32[2,128]{1,0:T(2,128)} %bitcast.6, ...), custom_call_target="tpu_custom_call" | custom-call | flops 60000002048 | bytes 20000000 | tf_op jit(solution)/shard_map/whole/pallas_call | solution.py:491
  92.7 1.7 %copy.14 = f32[256,256]{1,0:T(8,128)} copy(f32[256,256]{1,0:T(8,128)} %get-tuple-element.6) | data formatting | bytes 524288
  94.4 1.3 %copy.15 = f32[4,256]{1,0:T(4,128)} copy(f32[4,256]{1,0:T(4,128)} %get-tuple-element.7) | data formatting | bytes 8192
  95.6 2.3 %copy.16 = f32[64,4096]{1,0:T(8,128)} copy(f32[64,4096]{1,0:T(8,128)} %get-tuple-element.8) | data formatting | bytes 2097152

commit v5 on v4

--- a/solution.py
+++ b/solution.py
@@ -158,11 +158,11 @@
     return jnp.where(level == bucket, 2.0 * sign - 1.0, 0.0).astype(jnp.bfloat16)
 
 
-def whole_kernel(slab, omega, y_prev, w_prev, prev_bucket, prev_sign, slab_bucket, slab_sign, q_prev, q_new, x_core,
+def whole_kernel(slab, omega, y_in, w_prev, pb_in, ps_in, sb_in, ss_in, q_prev, q_new, x_core,
                  out, slab_v, omega_v, w_v, stack, part, got_sums, got_part, chip_sums, chip_part, got_a, got_b, got_s,
                  got_c, got_z, mid_p, mid_a, mid_s, xg, xs, u, us, ys, zs, ts, comb, comb_v, core, mapping,
                  early, v_far, v_up, v_down, terms, far_l, far_r, near_l, near_r, found_v, pass_up, pass_down,
-                 load_sem, swap_sem, a_sem, b_sem, s_sem, c_sem, z_sem, d_sem, e_sem, f_sem, g_sem, v_sem, x_sem, far_sem, near_sem):
+                 y_prev, prev_bucket, prev_sign, slab_bucket, slab_sign, small_sem, load_sem, swap_sem, a_sem, b_sem, s_sem, c_sem, z_sem, d_sem, e_sem, f_sem, g_sem, v_sem, x_sem, far_sem, near_sem):
     z, x, c, y = (lax.axis_index(name) for name in ("z", "x", "core", "y"))
 
     def at(dz=0, dx=0, dc=0, dy=0):
@@ -181,6 +181,14 @@
     for peer in peers:
         pl.semaphore_signal(barrier, inc=1, device_id=peer, device_id_type=MESH)
 
+    small = [
+        pltpu.make_async_copy(src, dst, small_sem.at[i])
+        for i, (src, dst) in enumerate(
+            zip((y_in, pb_in, ps_in, sb_in, ss_in), (y_prev, prev_bucket, prev_sign, slab_bucket, slab_sign))
+        )
+    ]
+    for copy in small:
+        copy.start()
     chunks = slab_v.shape[0]
     loads = []
     for i in range(chunks):
@@ -190,6 +198,9 @@
         load.start()
     for i in range(chunks):
         pltpu.make_async_copy(w_prev.at[:, pl.ds(i * CHUNK, CHUNK)], w_v.at[i], load_sem.at[2, i]).start()
+
+    for copy in small:
+        copy.wait()
 
     def real(ref):
         return ref[...].astype(jnp.float32)
@@ -342,8 +353,6 @@
         marks = out[0, yy, 0, PIECE + 2 * PART_B :, :]
         for h in (0, 1):
             ts[yy, :, 128 * h : 128 * h + 128] = table_of(marks[h : h + 1], marks[h + 2 : h + 3])
-    new = ys[...]
-    xg[...] = zs[L:, :] + mm(new, new, ((0,), (0,)))
     sketch = zs[:L, :]
     for yy in range(NY):
         sketch = sketch + signed_sum(ts[yy], ys[256 * yy : 256 * yy + 256, :])
@@ -390,6 +399,8 @@
         early[3, back, :] = early[3, back, :] + v_far[1]
         moves.append(along(early.at[3, back, :], v_down.at[back, :], v_sem, 5, 3))
 
+    new = ys[...]
+    xg[...] = zs[L:, :] + mm(new, new, over)
     xs[...] = mm(sketch, sketch, over)
     factor_both(xg, xs, u, us, after)
     row = lax.broadcasted_iota(jnp.int32, (K, K), 0)
@@ -475,6 +486,11 @@
         copy.wait_send()
 
 
+def hand_over(*refs):
+    for source, target in zip(refs[:3], refs[3:]):
+        target[...] = source[...]
+
+
 def whole(slab, omega, y_prev, w_prev, *marks):
     rows, cols = slab.shape
     chunks = cols // CHUNK
@@ -488,14 +504,14 @@
     def buffers(*shapes):
         return [pltpu.VMEM(shape, f32) for shape in shapes]
 
-    return pl.pallas_call(
+    found = pl.pallas_call(
         whole_kernel,
         out_shape=(
             jax.ShapeDtypeStruct(y_prev.shape, f32),
             jax.ShapeDtypeStruct((4, K), f32),
             jax.ShapeDtypeStruct((share, cols), f32),
         ),
-        in_specs=[hbm, hbm, vmem, hbm] + [vmem] * 4,
+        in_specs=[hbm] * 8,
         out_specs=[vmem] * 3,
         scratch_shapes=buffers(
             (NC, NY, NX, BLOCK, 128),
@@ -541,8 +557,11 @@
             (K, CHUNK),
             (share, CHUNK // 2),
             (share, CHUNK // 2),
+            y_prev.shape,
         )
+        + [pltpu.VMEM((2, 128), jnp.int32)] * 4
         + [
+            dma((5,)),
             dma((3, chunks)),
             dma((2, 2)),
             dma((2, 6)),
@@ -563,6 +582,13 @@
         cost_estimate=pl.CostEstimate(flops=60_000_000_000, bytes_accessed=20_000_000, transcendentals=0),
         name="whole",
     )(slab, omega, y_prev, w_prev, *(mark.reshape(2, 128) for mark in marks))
+    return pl.pallas_call(
+        hand_over,
+        out_shape=[jax.ShapeDtypeStruct(part.shape, f32) for part in found],
+        in_specs=[vmem] * 3,
+        out_specs=[vmem] * 3,
+        name="hand_over",
+    )(*found)
 
 
 def solution(mesh):

time: 98.1 us -> 98.8 us (level)
  Pallas kernels: 92 us -> 98 us
  local copies, waits for them, and re-layouts: 5.21 us -> 0 us
    unnamed x3 -> x0, local copies, waits for them, and re-layouts: 5.21 us -> none
    pallas_call x1, Pallas kernels: 92 us -> 95.6 us  [whole(): pl.pallas_call(whole_kernel, out_shape=(jax.ShapeDtypeStruct(y_prev.shape...]
    pallas_call x0 -> x1, Pallas kernels: none -> 2.39 us  [whole(): pl.pallas_call(hand_over, out_shape=[jax.ShapeDtypeStruct(part.shape, f32...]
where the time goes in v5:
time: 98.8 us; the launch traced here: 98.7 us
  Pallas kernels  98 us (99%)
    pallas_call x1, Pallas kernels, whole(): pl.pallas_call(whole_kernel, out_shape=(jax.ShapeDtypeStruct(y_prev.shape...  95.6 us
    pallas_call x1, Pallas kernels, whole(): pl.pallas_call(hand_over, out_shape=[jax.ShapeDtypeStruct(part.shape, f32...  2.39 us

profile of v5, /device:TPU:1, one launch (start us, length us, event | category | flops | bytes accessed | tf_op | source)
XLA Modules:
  0.0 98.7 jit_solution(4922308025440312511)
XLA Ops:
  0.6 95.6 %whole.1 = (f32[256,256]{1,0:T(8,128)}, f32[4,256]{1,0:T(4,128)}, f32[64,4096]{1,0:T(8,128)}) custom-call(f32[256,4096]{1,0:T(8,128)} %slab.1, f32[4096,256]{1,0:T(8,128)} %omega.1, f32[256,256]{1,0:T(8,128)} %y_in.1, f32[128,4096]{1,0:T(8,128)} %w_prev.1, s32[2,128]{1,0:T(2,128)} %bitcast.4, s32[2,128]{1,0:T(2,128)} %bitcast.5, s32[2,128]{1,0:T(2,128)} %bitcast.6, ...), custom_call_target="tpu_custom_call" | custom-call | flops 60000002048 | bytes 20000000 | tf_op jit(solution)/shard_map/whole/pallas_call | solution.py:507
  96.3 2.4 %hand_over.1 = (f32[256,256]{1,0:T(8,128)}, f32[4,256]{1,0:T(4,128)}, f32[64,4096]{1,0:T(8,128)}) custom-call(f32[256,256]{1,0:T(8,128)} %get-tuple-element.6.refs_0_, f32[4,256]{1,0:T(4,128)} %get-tuple-element.7.refs_1_, f32[64,4096]{1,0:T(8,128)} %get-tuple-element.8.refs_2_), custom_call_target="tpu_custom_call" | custom-call | tf_op jit(solution)/shard_map/hand_over/pallas_call | solution.py:585

commit v6 on v4

--- a/solution.py
+++ b/solution.py
@@ -475,6 +475,11 @@
         copy.wait_send()
 
 
+def hand_over(*refs):
+    for source, target in zip(refs[:3], refs[3:]):
+        target[...] = source[...]
+
+
 def whole(slab, omega, y_prev, w_prev, *marks):
     rows, cols = slab.shape
     chunks = cols // CHUNK
@@ -488,7 +493,7 @@
     def buffers(*shapes):
         return [pltpu.VMEM(shape, f32) for shape in shapes]
 
-    return pl.pallas_call(
+    found = pl.pallas_call(
         whole_kernel,
         out_shape=(
             jax.ShapeDtypeStruct(y_prev.shape, f32),
@@ -563,6 +568,13 @@
         cost_estimate=pl.CostEstimate(flops=60_000_000_000, bytes_accessed=20_000_000, transcendentals=0),
         name="whole",
     )(slab, omega, y_prev, w_prev, *(mark.reshape(2, 128) for mark in marks))
+    return pl.pallas_call(
+        hand_over,
+        out_shape=[jax.ShapeDtypeStruct(part.shape, f32) for part in found],
+        in_specs=[vmem] * 3,
+        out_specs=[vmem] * 3,
+        name="hand_over",
+    )(*found)
 
 
 def solution(mesh):

time: 98.1 us -> 95.2 us (0.970)
  local copies, waits for them, and re-layouts: 5.21 us -> 0 us
  Pallas kernels: 92 us -> 94.4 us
    unnamed x3 -> x0, local copies, waits for them, and re-layouts: 5.21 us -> none
    pallas_call x0 -> x1, Pallas kernels: none -> 2.39 us  [whole(): pl.pallas_call(hand_over, out_shape=[jax.ShapeDtypeStruct(part.shape, f32...]
where the time goes in v6:
time: 95.2 us; the launch traced here: 95.1 us
  Pallas kernels  94.4 us (99%)
    pallas_call x1, Pallas kernels, whole(): pl.pallas_call(whole_kernel, out_shape=(jax.ShapeDtypeStruct(y_prev.shape...  92 us
    pallas_call x1, Pallas kernels, whole(): pl.pallas_call(hand_over, out_shape=[jax.ShapeDtypeStruct(part.shape, f32...  2.39 us

profile of v6, /device:TPU:1, one launch (start us, length us, event | category | flops | bytes accessed | tf_op | source)
XLA Modules:
  0.0 95.1 jit_solution(13202430633613215934)
XLA Ops:
  0.6 92.0 %whole.1 = (f32[256,256]{1,0:T(8,128)}, f32[4,256]{1,0:T(4,128)}, f32[64,4096]{1,0:T(8,128)}) custom-call(f32[256,4096]{1,0:T(8,128)} %slab.1, f32[4096,256]{1,0:T(8,128)} %omega.1, f32[256,256]{1,0:T(8,128)} %y_prev.1, f32[128,4096]{1,0:T(8,128)} %w_prev.1, s32[2,128]{1,0:T(2,128)} %bitcast.4, s32[2,128]{1,0:T(2,128)} %bitcast.5, s32[2,128]{1,0:T(2,128)} %bitcast.6, ...), custom_call_target="tpu_custom_call" | custom-call | flops 60000002048 | bytes 20000000 | tf_op jit(solution)/shard_map/whole/pallas_call | solution.py:496
  92.7 2.4 %hand_over.1 = (f32[256,256]{1,0:T(8,128)}, f32[4,256]{1,0:T(4,128)}, f32[64,4096]{1,0:T(8,128)}) custom-call(f32[256,256]{1,0:T(8,128)} %get-tuple-element.6.refs_0_, f32[4,256]{1,0:T(4,128)} %get-tuple-element.7.refs_1_, f32[64,4096]{1,0:T(8,128)} %get-tuple-element.8.refs_2_), custom_call_target="tpu_custom_call" | custom-call | tf_op jit(solution)/shard_map/hand_over/pallas_call | solution.py:571
